TPU v7x, 16 devices: a whole 2x2x2 slice. The times are simulated.
16 devices in a mesh: model: 2 (over z), data: 8 (over y, x, core).
Axes of the slice: x: 2, y: 2, z: 2, core: 2. Of those that a mesh axis runs over, the one named last changes fastest.
Arguments:
- local_grads: bfloat16 [8, 12, 2359296], P('data', None, 'model')
- master: float32 [12, 2359296], P(None, ('model', 'data'))
- moment_one: float32 [12, 2359296], P(None, ('model', 'data'))
- moment_two: float32 [12, 2359296], P(None, ('model', 'data'))
Outputs:
- output 1: bfloat16 [12, 2359296], P(None, 'model')
- output 2: float32 [12, 2359296], P(None, ('model', 'data'))
- output 3: float32 [12, 2359296], P(None, ('model', 'data'))
- output 4: float32 [12, 2359296], P(None, ('model', 'data'))
All inputs are finite; a program needn't handle non-finite values.
Results may differ from a plain program's by a relative error of at most 0.001.
Values are sent between devices in bfloat16 or wider.
A program may use at most 1 GiB of HBM per device.

v0:
```python
import jax
import jax.numpy as jnp
from jax import lax
from jax.sharding import PartitionSpec as P

STEP = 4
LEARN_RATE = 0.08
BETA_ONE = 0.9
BETA_TWO = 0.999
EPSILON = 1e-6
WEIGHT_DECAY = 0.01
MAX_NORM = 1.0
CORR_ONE = 1.0 - BETA_ONE ** STEP
CORR_TWO = 1.0 - BETA_TWO ** STEP


def tensor_sums(block_values):
    return jnp.stack([block_values[..., 0:3].sum(axis=-1), block_values[..., 3], block_values[..., 4:8].sum(axis=-1), block_values[..., 8:12].sum(axis=-1)], axis=-1)


def spread_tensors(tensor_values):
    lead_shape = tensor_values.shape[:-1]
    pieces = [jnp.broadcast_to(tensor_values[..., tensor_pos:tensor_pos + 1], lead_shape + (block_count,)) for tensor_pos, block_count in enumerate((3, 1, 4, 4))]
    return jnp.concatenate(pieces, axis=-1)


def adam_direction(grad_mean, clip_scale, master, moment_one, moment_two):
    scaled = clip_scale * grad_mean
    new_one = BETA_ONE * moment_one + (1.0 - BETA_ONE) * scaled
    new_two = BETA_TWO * moment_two + (1.0 - BETA_TWO) * scaled * scaled
    direction = (new_one / CORR_ONE) / (jnp.sqrt(new_two / CORR_TWO) + EPSILON) + WEIGHT_DECAY * master
    return new_one, new_two, direction


def block_ratio(norm_sq):
    tensor_norms = jnp.sqrt(tensor_sums(norm_sq.reshape(2, -1, 12)))
    return spread_tensors(tensor_norms[0] / tensor_norms[1]).reshape(-1, 1)


def solution(mesh):
    data_size = mesh.shape['data']
    both_axes = ('model', 'data')
    state_spec = P(None, both_axes)

    def device_step(local_grads, master, moment_one, moment_two):
        grad_slab = local_grads[0]
        received = lax.all_to_all(grad_slab, 'data', 1, 0, tiled=True)
        grad_mean = jnp.sum(received.reshape(data_size, grad_slab.shape[0], -1), axis=0, dtype=jnp.float32) / data_size
        total_sq = lax.psum(jnp.sum(grad_mean * grad_mean), both_axes)
        clip_scale = jnp.minimum(1.0, MAX_NORM / jnp.sqrt(total_sq))
        new_one, new_two, direction = adam_direction(grad_mean, clip_scale, master, moment_one, moment_two)
        norm_sq = lax.psum(jnp.stack([jnp.sum(master * master, axis=1), jnp.sum(direction * direction, axis=1)]), both_axes)
        new_master = master - LEARN_RATE * block_ratio(norm_sq) * direction
        params = lax.all_gather(new_master.astype(jnp.bfloat16), 'data', axis=1, tiled=True)
        return params, new_master, new_one, new_two

    return jax.shard_map(device_step, mesh=mesh, in_specs=(P('data', None, 'model'), state_spec, state_spec, state_spec), out_specs=(P(None, 'model'), state_spec, state_spec, state_spec), check_vma=False)
```

profile of v0, /device:TPU:0, one launch (start us, length us, event | category | flops | bytes accessed | tf_op | source)
XLA Modules:
  0.0 848.1 jit_solution(10487742766353150651)
XLA Ops:
  7.2 0.0 all-gather.2.cloned.1.call-start
  7.2 32.6 %copy.18 = bf16[2,8,8,147456]{3,2,1,0:T(8,128)(2,1)} copy(bf16[2,8,8,147456]{3,1,2,0:T(8,128)(2,1)} %bitcast.33) | data formatting | bytes 75497472
  39.8 19.4 %slice.40 = bf16[12,8,147456]{2,1,0:T(8,128)(2,1)} slice(bf16[16,8,147456]{2,1,0:T(8,128)(2,1)} %bitcast.32), slice={[0:12], [0:8], [0:147456]} | slice | bytes 56623104 | tf_op jit(solution)/shard_map/all_to_all | solution.py:47
  59.2 27.5 %copy.14 = bf16[12,8,147456]{2,0,1:T(8,128)(2,1)} copy(bf16[12,8,147456]{2,1,0:T(8,128)(2,1)} %slice.40) | data formatting | bytes 56623104 | tf_op jit(solution)/shard_map/all_to_all | solution.py:47
  86.7 421.3 %all_to_all.13 = bf16[12,8,147456]{2,0,1:T(8,128)(2,1)} all-to-all(bf16[12,8,147456]{2,0,1:T(8,128)(2,1)} %copy.14), channel_id=1, replica_groups=mesh['model'=2,'data'=8] {'data'}, dimensions={1} | all-to-all | bytes 56623104 | tf_op jit(solution)/shard_map/all_to_all | solution.py:47
  508.0 16.8 %convert_reduce_fusion = f32[12,147456]{1,0:T(8,128)} fusion(bf16[12,8,147456]{2,0,1:T(8,128)(2,1)} %all_to_all.13), kind=kLoop, calls=%fused_computation | loop fusion | flops 26542080 | bytes 35389440 | tf_op jit(solution)/shard_map/reduce_sum | solution.py:48
  524.9 5.6 multiply_reduce_fusion.1
  530.5 32.7 %psum.14 = f32[]{:T(128)} all-reduce(f32[]{:T(128)} %multiply_reduce_fusion.1), channel_id=1, replica_groups=mesh['model'=2,'data'=8] {'model','data'}, use_global_device_ids=true, to_apply=%region_3.0 | all-reduce | flops 1 | bytes 8 | tf_op jit(solution)/shard_map/psum | solution.py:49
  563.9 22.3 %multiply_reduce_fusion.2 = (f32[12]{0:T(128)S(1)}, f32[12]{0:T(128)S(1)}, f32[12,147456]{1,0:T(8,128)}, f32[12,147456]{1,0:T(8,128)}) fusion(f32[12,147456]{1,0:T(8,128)} %param.5, f32[12,147456]{1,0:T(8,128)} %convert_reduce_fusion, f32[]{:T(128)S(6)} %mul.73, f32[12,147456]{1,0:T(8,128)} %param.6, f32[12,147456]{1,0:T(8,128)} %param.7), kind=kLoop, calls=%fused_computation.8 | loop fusion | flops 31850472 | bytes 42467428 | tf_op jit(solution)/shard_map/reduce_sum | solution.py:52
  586.2 32.9 %psum.15 = f32[2,1,12]{2,0,1:T(2,128)S(1)} all-reduce(f32[2,1,12]{2,0,1:T(2,128)S(1)} %maximum_bitcast_fusion), channel_id=1, replica_groups=mesh['model'=2,'data'=8] {'model','data'}, use_global_device_ids=true, to_apply=%region_5.0 | all-reduce | flops 24 | bytes 192 | tf_op jit(solution)/shard_map/psum | solution.py:52
  619.1 0.1 slice_reduce_fusion.2
  619.2 0.1 slice.31
  619.2 0.2 slice_reduce_fusion.1
  619.5 0.1 copy.15
  619.5 0.1 copy.17
  619.6 0.1 copy.16
  619.7 0.1 maximum_sqrt_fusion
  619.8 0.7 fusion.6
  620.5 0.6 broadcast_in_dim.26
  621.2 0.7 broadcast_in_dim.24
  621.9 0.6 broadcast_in_dim.22
  622.4 0.7 fusion.2
  623.2 16.7 %fusion.4 = (bf16[12,147456]{1,0:T(8,128)(2,1)}, f32[12,147456]{1,0:T(8,128)}) fusion(f32[12,147456]{1,0:T(8,128)} %param.5, f32[12,147456]{1,0:T(8,128)} %get-tuple-element.23, f32[12,147456]{1,0:T(8,128)} %get-tuple-element.22, f32[12]{0:T(128)S(1)} %fusion.2), kind=kLoop, calls=%fused_computation.21 | loop fusion | flops 15925248 | bytes 31850544 | tf_op jit(solution)/shard_map/convert_element_type | solution.py:54
  639.8 0.0 all-gather.2.cloned.1.call-update
  639.8 176.0 %all-gather.2.cloned.1.call-done = bf16[12,1179648]{1,0:T(8,128)(2,1)} async-done(((bf16[12,147456]{1,0:T(8,128)(2,1)}), bf16[12,1179648]{1,0:T(8,128)(2,1)}) %all-gather.2.cloned.1.call-update) | async-done | bytes 28311568 | tf_op jit(solution)/shard_map/all_gather | solution.py:54
  815.8 25.4 %copy.20 = bf16[12,1179648]{1,0:T(8,128)(2,1)} copy(bf16[12,1179648]{1,0:T(8,128)(2,1)} %all-gather.2.cloned.1.call-done) | data formatting | bytes 56623104
  (2 shorter events, 0.0 us)
Async XLA Ops:
  7.2 808.6 %all-gather.2.cloned.1.call-start = ((), (), s32[]{:S(2)}) async-start(), calls=%async_computation.1 | async-start | bytes 42467328 | tf_op jit(solution)/shard_map/all_gather | solution.py:54
Sparse Core Ops, SparseCore 0:
  640.0 175.7 all-gather.1
where the time goes:
time: 849 us; the launch traced here: 848 us
  blocking collectives  487 us (57%)
  waiting for transfers between devices  176 us (21%)
  local copies, waits for them, and re-layouts  108 us (13%)
  other arithmetic  62.5 us (7%)
  between operations  14.8 us (2%)
    all_to_all x1, blocking collectives, device_step(): received = lax.all_to_all(grad_slab, 'data', 1, 0, tiled=True)  421 us
    all_gather x1, waiting for transfers between devices, device_step(): lax.all_gather(new_master.astype(jnp.bfloat16), 'data', axis=1, tiled=True)  176 us
    unnamed x2, local copies, waits for them, and re-layouts  58 us
    all_to_all x2, local copies, waits for them, and re-layouts, device_step(): received = lax.all_to_all(grad_slab, 'data', 1, 0, tiled=True)  46.9 us
    psum x1, blocking collectives, device_step(): lax.psum(jnp.stack([jnp.sum(master * master, axis=1), jnp.sum(direction *...  32.9 us
    psum x1, blocking collectives, device_step(): total_sq = lax.psum(jnp.sum(grad_mean * grad_mean), both_axes)  32.7 us
    reduce_sum x1, other arithmetic, device_step(): jnp.sum(master * master, axis=1)  22.3 us
  transfers between devices with their start and end apart: 1, of which 1 were waited for; matrix products, arithmetic and copies ran while one was open for 0% of the time, Pallas kernels for 0%

commit v1 on v0

--- a/solution.py
+++ b/solution.py
@@ -1,6 +1,10 @@
+import functools
+
 import jax
 import jax.numpy as jnp
 from jax import lax
+from jax.experimental import pallas as pl
+from jax.experimental.pallas import tpu as pltpu
 from jax.sharding import PartitionSpec as P
 
 STEP = 4
@@ -13,6 +17,187 @@
 CORR_ONE = 1.0 - BETA_ONE ** STEP
 CORR_TWO = 1.0 - BETA_TWO ** STEP
 
+MESH = pl.DeviceIdType.MESH
+F32 = jnp.float32
+BF16 = jnp.bfloat16
+
+SHARD = 147456
+COLS = 12288
+TOP_ROUTE = SHARD // 2
+BOT_ROUTE = SHARD // 4
+N_TOP = TOP_ROUTE // COLS
+N_BOT = BOT_ROUTE // COLS
+N_CHUNK = N_TOP + N_BOT
+STRIP = 512
+
+
+def flip(value):
+    return 1 - value
+
+
+def my_place():
+    data_pos = lax.axis_index('data')
+    return data_pos // 4, lax.rem(data_pos // 2, 2), lax.rem(data_pos, 2)
+
+
+def data_index(pos_y, pos_x, core):
+    return (pos_y * 2 + pos_x) * 2 + core
+
+
+def others():
+    mine = lax.axis_index('model') * 8 + lax.axis_index('data')
+    for step in range(1, 16):
+        other = lax.rem(mine + step, 16)
+        yield other // 8, lax.rem(other, 8)
+
+
+def enter_all():
+    barrier = pltpu.get_barrier_semaphore()
+    for device in others():
+        pl.semaphore_signal(barrier, inc=1, device_id=device, device_id_type=MESH)
+    pl.semaphore_wait(barrier, 15)
+
+
+def drain(ref, sem):
+    pltpu.make_async_copy(ref, ref, sem).wait()
+
+
+def share_all(box, send_sem, recv_sem):
+    mine = lax.axis_index('model') * 8 + lax.axis_index('data')
+    for device in others():
+        pltpu.make_async_remote_copy(src_ref=box.at[mine], dst_ref=box.at[mine], send_sem=send_sem, recv_sem=recv_sem, device_id=device, device_id_type=MESH).start()
+    drain(box.at[pl.ds(0, 15)], send_sem)
+    drain(box.at[pl.ds(0, 15)], recv_sem)
+
+
+def chunk_views(array, shard, route, chunk, block, top):
+    if top:
+        start = pl.multiple_of(shard * SHARD + route * TOP_ROUTE + chunk * COLS, COLS)
+        return [(array.at[pl.ds(0, 8), pl.ds(start, COLS)], block)]
+    views = []
+    for half in range(2):
+        start = pl.multiple_of(shard * SHARD + half * TOP_ROUTE + route * BOT_ROUTE + (chunk - N_TOP) * COLS, COLS)
+        views.append((array.at[pl.ds(8, 4), pl.ds(start, COLS)], block.at[pl.ds(4 * half, 4)]))
+    return views
+
+
+def reduce_kernel(grads, mean_out, total_out, first, sent, got, kept, box, first_send, first_recv, second_send, second_recv, out_sem, box_send, box_recv):
+    pos_y, pos_x, core = my_place()
+    model_pos = lax.axis_index('model')
+    grad = grads.at[0]
+
+    def local(chunk, top):
+        for route in range(2):
+            for far in range(2):
+                row, col = ((lax.rem(pos_y + far, 2), pos_x), (pos_y, lax.rem(pos_x + far, 2)))[route]
+                shard = data_index(row, col, core)
+                for src, dst in chunk_views(grad, shard, route, chunk, first.at[route, chunk, 0, far], top):
+                    pltpu.make_async_copy(src, dst, first_recv.at[route, chunk]).start()
+
+    def remote(chunk, top):
+        for far in range(2):
+            for other in range(2):
+                for route in range(2):
+                    side = (pos_y, flip(pos_x)) if route == 0 else (flip(pos_y), pos_x)
+                    to_core = lax.rem(core + other, 2)
+                    row, col = (lax.rem(side[0] + far, 2), side[1]) if route == 0 else (side[0], lax.rem(side[1] + far, 2))
+                    for src, dst in chunk_views(grad, data_index(row, col, to_core), route, chunk, first.at[route, chunk, 2 + other, far], top):
+                        pltpu.make_async_remote_copy(src_ref=src, dst_ref=dst, send_sem=first_send.at[route, chunk], recv_sem=first_recv.at[route, chunk], device_id=(model_pos, data_index(side[0], side[1], to_core)), device_id_type=MESH).start()
+            for route in range(2):
+                row, col = ((lax.rem(pos_y + far, 2), pos_x), (pos_y, lax.rem(pos_x + far, 2)))[route]
+                for src, dst in chunk_views(grad, data_index(row, col, flip(core)), route, chunk, first.at[route, chunk, 1, far], top):
+                    pltpu.make_async_remote_copy(src_ref=src, dst_ref=dst, send_sem=first_send.at[route, chunk], recv_sem=first_recv.at[route, chunk], device_id=(model_pos, data_index(pos_y, pos_x, flip(core))), device_id_type=MESH).start()
+
+    def over_chunks(body):
+        pl.loop(0, N_TOP)(functools.partial(body, top=True))
+        pl.loop(N_TOP, N_CHUNK)(functools.partial(body, top=False))
+
+    over_chunks(local)
+    enter_all()
+    over_chunks(remote)
+
+    def second(route, chunk):
+        side = data_index(flip(pos_y), pos_x, core) if route == 0 else data_index(pos_y, flip(pos_x), core)
+        return pltpu.make_async_remote_copy(src_ref=sent.at[route, chunk], dst_ref=got.at[route, chunk], send_sem=second_send.at[route, chunk], recv_sem=second_recv.at[route, chunk], device_id=(model_pos, side), device_id_type=MESH)
+
+    def add_four(route, chunk):
+        drain(first.at[route, chunk], first_recv.at[route, chunk])
+
+        @pl.loop(0, COLS // STRIP)
+        def _(strip):
+            cols = pl.ds(pl.multiple_of(strip * STRIP, STRIP), STRIP)
+            for far, target in ((0, kept), (1, sent)):
+                parts = [first[route, chunk, source, far, :, cols].astype(F32) for source in range(4)]
+                target[route, chunk, :, cols] = (parts[0] + parts[1]) + (parts[2] + parts[3])
+
+    @pl.loop(0, N_CHUNK)
+    def _(chunk):
+        add_four(0, chunk)
+
+        @pl.when(chunk > 0)
+        def _():
+            second(1, chunk - 1).start()
+
+        add_four(1, chunk)
+        second(0, chunk).start()
+
+    second(1, N_CHUNK - 1).start()
+
+    def writes(route, chunk, top):
+        return [pltpu.make_async_copy(block, view, out_sem.at[route, chunk]) for view, block in chunk_views(mean_out, 0, route, chunk, kept.at[route, chunk], top)]
+
+    def finish(chunk, squares, top):
+        for route in range(2):
+            drain(got.at[route, chunk], second_recv.at[route, chunk])
+
+            def strip_body(strip, total):
+                cols = pl.ds(pl.multiple_of(strip * STRIP, STRIP), STRIP)
+                mean = (kept[route, chunk, :, cols] + got[route, chunk, :, cols]) * 0.125
+                kept[route, chunk, :, cols] = mean
+                square = mean * mean
+                for tile in range(STRIP // 128):
+                    total = total + square[:, tile * 128:(tile + 1) * 128]
+                return total
+
+            squares = lax.fori_loop(0, COLS // STRIP, strip_body, squares)
+            for copy in writes(route, chunk, top):
+                copy.start()
+        return squares
+
+    squares = lax.fori_loop(0, N_TOP, functools.partial(finish, top=True), jnp.zeros((8, 128), F32))
+    squares = lax.fori_loop(N_TOP, N_CHUNK, functools.partial(finish, top=False), squares)
+    box[model_pos * 8 + lax.axis_index('data')] = squares
+    share_all(box, box_send, box_recv)
+    total_out[...] = jnp.sum(box[...], axis=0)
+
+    @pl.loop(0, N_CHUNK)
+    def _(chunk):
+        for route in range(2):
+            drain(first.at[route, chunk, pl.ds(1, 3)], first_send.at[route, chunk])
+            drain(sent.at[route, chunk], second_send.at[route, chunk])
+            drain(kept.at[route, chunk], out_sem.at[route, chunk])
+
+
+def reduce_grads(local_grads):
+    sems = pltpu.SemaphoreType.DMA((2, N_CHUNK))
+    return pl.pallas_call(
+        reduce_kernel,
+        out_shape=(jax.ShapeDtypeStruct((12, SHARD), F32), jax.ShapeDtypeStruct((8, 128), F32)),
+        in_specs=[pl.BlockSpec(memory_space=pltpu.HBM)],
+        out_specs=(pl.BlockSpec(memory_space=pltpu.HBM), pl.BlockSpec(memory_space=pltpu.VMEM)),
+        scratch_shapes=[
+            pltpu.VMEM((2, N_CHUNK, 4, 2, 8, COLS), BF16),
+            pltpu.VMEM((2, N_CHUNK, 8, COLS), F32),
+            pltpu.VMEM((2, N_CHUNK, 8, COLS), F32),
+            pltpu.VMEM((2, N_CHUNK, 8, COLS), F32),
+            pltpu.VMEM((16, 8, 128), F32),
+            sems, sems, sems, sems, sems,
+            pltpu.SemaphoreType.DMA, pltpu.SemaphoreType.DMA,
+        ],
+        compiler_params=pltpu.CompilerParams(collective_id=0, has_side_effects=True, vmem_limit_bytes=60 * 1024 * 1024),
+        name='reduce_grads',
+    )(local_grads)
+
 
 def tensor_sums(block_values):
     return jnp.stack([block_values[..., 0:3].sum(axis=-1), block_values[..., 3], block_values[..., 4:8].sum(axis=-1), block_values[..., 8:12].sum(axis=-1)], axis=-1)
@@ -38,16 +223,12 @@
 
 
 def solution(mesh):
-    data_size = mesh.shape['data']
     both_axes = ('model', 'data')
     state_spec = P(None, both_axes)
 
     def device_step(local_grads, master, moment_one, moment_two):
-        grad_slab = local_grads[0]
-        received = lax.all_to_all(grad_slab, 'data', 1, 0, tiled=True)
-        grad_mean = jnp.sum(received.reshape(data_size, grad_slab.shape[0], -1), axis=0, dtype=jnp.float32) / data_size
-        total_sq = lax.psum(jnp.sum(grad_mean * grad_mean), both_axes)
-        clip_scale = jnp.minimum(1.0, MAX_NORM / jnp.sqrt(total_sq))
+        grad_mean, total = reduce_grads(local_grads)
+        clip_scale = jnp.minimum(1.0, MAX_NORM / jnp.sqrt(jnp.sum(total)))
         new_one, new_two, direction = adam_direction(grad_mean, clip_scale, master, moment_one, moment_two)
         norm_sq = lax.psum(jnp.stack([jnp.sum(master * master, axis=1), jnp.sum(direction * direction, axis=1)]), both_axes)
         new_master = master - LEARN_RATE * block_ratio(norm_sq) * direction

time: 849 us -> 533 us (0.63)
  blocking collectives: 487 us -> 31.9 us
  Pallas kernels: 0 us -> 240 us
  local copies, waits for them, and re-layouts: 108 us -> 28.3 us
  other arithmetic: 62.5 us -> 41.4 us
    all_to_all x1 -> x0, blocking collectives: 421 us -> none  [device_step(): received = lax.all_to_all(grad_slab, 'data', 1, 0, tiled=True)]
    pallas_call x0 -> x1, Pallas kernels: none -> 240 us  [reduce_grads(): pl.pallas_call(reduce_kernel, out_shape=(jax.ShapeDtypeStruct((12, SHARD)...]
    all_to_all x2 -> x0, local copies, waits for them, and re-layouts: 46.9 us -> none  [device_step(): received = lax.all_to_all(grad_slab, 'data', 1, 0, tiled=True)]
    psum x1 -> x0, blocking collectives: 32.7 us -> none  [device_step(): total_sq = lax.psum(jnp.sum(grad_mean * grad_mean), both_axes)]
    unnamed x2 -> x1, local copies, waits for them, and re-layouts: 58 us -> 25.4 us
    reduce_sum x2 -> x1, other arithmetic: 22.4 us -> 1.29 us  [device_step(): clip_scale = jnp.minimum(1.0, MAX_NORM / jnp.sqrt(jnp.sum(total)))]
where the time goes in v1:
time: 533 us; the launch traced here: 532 us
  Pallas kernels  240 us (45%)
  waiting for transfers between devices  176 us (33%)
  other arithmetic  41.4 us (8%)
  blocking collectives  31.9 us (6%)
  local copies, waits for them, and re-layouts  28.3 us (5%)
  between operations  14.8 us (3%)
    pallas_call x1, Pallas kernels, reduce_grads(): pl.pallas_call(reduce_kernel, out_shape=(jax.ShapeDtypeStruct((12, SHARD)...  240 us
    all_gather x1, waiting for transfers between devices, device_step(): lax.all_gather(new_master.astype(jnp.bfloat16), 'data', axis=1, tiled=True)  176 us
    psum x1, blocking collectives, device_step(): lax.psum(jnp.stack([jnp.sum(master * master, axis=1), jnp.sum(direction *...  31.9 us
    unnamed x1, local copies, waits for them, and re-layouts  25.4 us
    reduce_sum x1, other arithmetic, device_step(): jnp.sum(master * master, axis=1)  22.3 us
    convert_element_type x1, other arithmetic, device_step(): new_master.astype(jnp.bfloat16)  16.7 us
  transfers between devices with their start and end apart: 1, of which 1 were waited for; matrix products, arithmetic and copies ran while one was open for 0% of the time, Pallas kernels for 0%

profile of v1, /device:TPU:0, one launch (start us, length us, event | category | flops | bytes accessed | tf_op | source)
XLA Modules:
  0.0 532.4 jit_solution(7242487433163140586)
XLA Ops:
  7.2 0.0 all-gather.2.cloned.1.call-start
  7.2 240.0 %reduce_grads.1 = (f32[12,147456]{1,0:T(8,128)}, f32[8,128]{1,0:T(8,128)}) custom-call(bf16[1,12,1179648]{2,1,0:T(8,128)(2,1)} %grads.1), custom_call_target="tpu_custom_call" | custom-call | tf_op jit(solution)/shard_map/reduce_grads/pallas_call | solution.py:183
  247.2 1.3 reduce_sum.55
  249.2 22.3 %multiply_reduce_fusion.1 = (f32[12]{0:T(128)S(1)}, f32[12]{0:T(128)S(1)}, f32[12,147456]{1,0:T(8,128)}, f32[12,147456]{1,0:T(8,128)}) fusion(f32[12,147456]{1,0:T(8,128)} %param.5, f32[12,147456]{1,0:T(8,128)} %get-tuple-element.7, f32[]{:T(128)S(6)} %min.3, f32[12,147456]{1,0:T(8,128)} %param.6, f32[12,147456]{1,0:T(8,128)} %param.7), kind=kLoop, calls=%fused_computation.6 | loop fusion | flops 31850472 | bytes 42467428 | tf_op jit(solution)/shard_map/reduce_sum | solution.py:233
  271.5 31.9 %psum.7 = f32[2,1,12]{2,0,1:T(2,128)S(1)} all-reduce(f32[2,1,12]{2,0,1:T(2,128)S(1)} %maximum_bitcast_fusion), channel_id=1, replica_groups=mesh['model'=2,'data'=8] {'model','data'}, use_global_device_ids=true, to_apply=%region_3.0 | all-reduce | flops 24 | bytes 192 | tf_op jit(solution)/shard_map/psum | solution.py:233
  303.4 0.1 slice_reduce_fusion.2
  303.5 0.1 slice.31
  303.6 0.2 slice_reduce_fusion.1
  303.8 0.1 copy.8
  303.9 0.1 copy.10
  304.0 0.1 copy.9
  304.1 0.1 maximum_sqrt_fusion
  304.2 0.7 fusion.6
  304.8 0.6 broadcast_in_dim.26
  305.5 0.7 broadcast_in_dim.24
  306.2 0.6 broadcast_in_dim.22
  306.8 0.7 fusion.2
  307.5 16.7 %fusion.4 = (bf16[12,147456]{1,0:T(8,128)(2,1)}, f32[12,147456]{1,0:T(8,128)}) fusion(f32[12,147456]{1,0:T(8,128)} %param.5, f32[12,147456]{1,0:T(8,128)} %get-tuple-element.27, f32[12,147456]{1,0:T(8,128)} %get-tuple-element.26, f32[12]{0:T(128)S(1)} %fusion.2), kind=kLoop, calls=%fused_computation.19 | loop fusion | flops 15925248 | bytes 31850544 | tf_op jit(solution)/shard_map/convert_element_type | solution.py:235
  324.1 0.0 all-gather.2.cloned.1.call-update
  324.2 176.0 %all-gather.2.cloned.1.call-done = bf16[12,1179648]{1,0:T(8,128)(2,1)} async-done(((bf16[12,147456]{1,0:T(8,128)(2,1)}), bf16[12,1179648]{1,0:T(8,128)(2,1)}) %all-gather.2.cloned.1.call-update) | async-done | bytes 28311568 | tf_op jit(solution)/shard_map/all_gather | solution.py:235
  500.1 25.4 %copy.12 = bf16[12,1179648]{1,0:T(8,128)(2,1)} copy(bf16[12,1179648]{1,0:T(8,128)(2,1)} %all-gather.2.cloned.1.call-done) | data formatting | bytes 56623104
  (2 shorter events, 0.0 us)
Async XLA Ops:
  7.2 493.0 %all-gather.2.cloned.1.call-start = ((), (), s32[]{:S(2)}) async-start(), calls=%async_computation | async-start | bytes 42467328 | tf_op jit(solution)/shard_map/all_gather | solution.py:235
Sparse Core Ops, SparseCore 0:
  324.3 175.7 all-gather.1

commit v2 on v0

v2 whole, which is shorter than its diff:
```python
import functools

import jax
import jax.numpy as jnp
from jax import lax
from jax.experimental import pallas as pl
from jax.experimental.pallas import tpu as pltpu
from jax.sharding import PartitionSpec as P

STEP = 4
LEARN_RATE = 0.08
BETA_ONE = 0.9
BETA_TWO = 0.999
EPSILON = 1e-6
WEIGHT_DECAY = 0.01
MAX_NORM = 1.0
CORR_ONE = 1.0 - BETA_ONE ** STEP
CORR_TWO = 1.0 - BETA_TWO ** STEP

MESH = pl.DeviceIdType.MESH
F32 = jnp.float32
BF16 = jnp.bfloat16

SHARD = 147456
COLS = 12288
TOP_ROUTE = SHARD // 2
BOT_ROUTE = SHARD // 4
N_TOP = TOP_ROUTE // COLS
N_BOT = BOT_ROUTE // COLS
N_CHUNK = N_TOP + N_BOT
STRIP = 512

MIB = 1024 * 1024
STEP_LIMIT = 9 * MIB
WRITE_LIMIT = STEP_LIMIT


def flip(value):
    return 1 - value


def my_place():
    data_pos = lax.axis_index('data')
    return data_pos // 4, lax.rem(data_pos // 2, 2), lax.rem(data_pos, 2)


def data_index(pos_y, pos_x, core):
    return (pos_y * 2 + pos_x) * 2 + core


def others():
    mine = lax.axis_index('model') * 8 + lax.axis_index('data')
    for step in range(1, 16):
        other = lax.rem(mine + step, 16)
        yield other // 8, lax.rem(other, 8)


def enter_all():
    barrier = pltpu.get_barrier_semaphore()
    for device in others():
        pl.semaphore_signal(barrier, inc=1, device_id=device, device_id_type=MESH)
    pl.semaphore_wait(barrier, 15)


def drain(ref, sem):
    pltpu.make_async_copy(ref, ref, sem).wait()


def row_views(array, shard, route, chunk, block, top):
    if top:
        start = shard * SHARD + route * TOP_ROUTE + chunk * COLS
        return [(array.at[pl.ds(0, 8), pl.ds(pl.multiple_of(start, COLS), COLS)], block)]
    views = []
    for half in range(2):
        start = shard * SHARD + half * TOP_ROUTE + route * BOT_ROUTE + (chunk - N_TOP) * COLS
        views.append((array.at[pl.ds(8, 4), pl.ds(pl.multiple_of(start, COLS), COLS)], block.at[pl.ds(4 * half, 4)]))
    return views


def sweep(body, carry=0):
    carry = lax.fori_loop(0, N_TOP, functools.partial(body, top=True), carry)
    return lax.fori_loop(N_TOP, N_CHUNK, functools.partial(body, top=False), carry)


def strips(body, carry=0):
    def step(strip, carry):
        return body(pl.ds(pl.multiple_of(strip * STRIP, STRIP), STRIP), carry)

    return lax.fori_loop(0, COLS // STRIP, step, carry)


def fold(total, values):
    for tile in range(STRIP // 128):
        total = total + values[:, tile * 128:(tile + 1) * 128]
    return total


def step_kernel(
    grads, master_in, one_in, two_in,
    top_out, bot_out, master, one, two,
    mean, total_box, norm_box,
    first_send, first_recv, second_send, second_recv, load_sem,
    side_send, side_recv, forward_send, corner_recv, partner_send, partner_recv, box_sem,
):
    pos_y, pos_x, core = my_place()
    model_pos = lax.axis_index('model')
    mine = model_pos * 8 + lax.axis_index('data')
    grad = grads.at[0]
    sent, got = master, two
    chips = ((pos_y, pos_x), (pos_y, flip(pos_x)), (flip(pos_y), pos_x), (flip(pos_y), flip(pos_x)))
    places = [data_index(row, col, core) for row, col in chips]
    partner = data_index(pos_y, pos_x, flip(core))

    def copy_to(src, dst, place, send_sem, recv_sem):
        pltpu.make_async_remote_copy(src_ref=src, dst_ref=dst, send_sem=send_sem, recv_sem=recv_sem, device_id=(model_pos, place), device_id_type=MESH).start()

    def landing(route, chunk, block, count, top):
        if top:
            start = ((route * N_TOP + chunk) * 8 + block) * COLS
        else:
            start = ((route * N_BOT + chunk - N_TOP) * 8 + block) * COLS
        return (top_out if top else bot_out).at[:, pl.ds(pl.multiple_of(start, COLS), count * COLS)]

    def wanted(route, row, col, far):
        return (lax.rem(row + far, 2), col) if route == 0 else (row, lax.rem(col + far, 2))

    def local(chunk, carry, top):
        for route in range(2):
            for far in range(2):
                shard = data_index(*wanted(route, pos_y, pos_x, far), core)
                for src, dst in row_views(grad, shard, route, chunk, landing(route, chunk, far, 1, top), top):
                    pltpu.make_async_copy(src, dst, first_recv.at[route, chunk]).start()
        return carry

    def remote(chunk, carry, top):
        for far in range(2):
            for other in range(2):
                for route in range(2):
                    row, col = chips[1 + route]
                    to_core = lax.rem(core + other, 2)
                    shard = data_index(*wanted(route, row, col, far), to_core)
                    for src, dst in row_views(grad, shard, route, chunk, landing(route, chunk, 4 + 2 * other + far, 1, top), top):
                        copy_to(src, dst, data_index(row, col, to_core), first_send.at[route, chunk], first_recv.at[route, chunk])
            for route in range(2):
                shard = data_index(*wanted(route, pos_y, pos_x, far), flip(core))
                for src, dst in row_views(grad, shard, route, chunk, landing(route, chunk, 2 + far, 1, top), top):
                    copy_to(src, dst, partner, first_send.at[route, chunk], first_recv.at[route, chunk])
        return carry

    def load(which, array, block, route, chunk, top):
        for src, dst in row_views(array, 0, route, chunk, block.at[route, chunk], top):
            pltpu.make_async_copy(src, dst, load_sem.at[which, route, chunk]).start()

    sweep(local)
    enter_all()
    sweep(remote)

    def load_one(chunk, carry, top):
        for route in range(2):
            load(1, one_in, one, route, chunk, top)
        return carry

    sweep(load_one)

    def second(route, chunk):
        copy_to(sent.at[route, chunk], got.at[route, chunk], places[2 - route], second_send.at[route, chunk], second_recv.at[route, chunk])

    def add_four(route, chunk, top):
        drain(landing(route, chunk, 0, 8, top), first_recv.at[route, chunk])

        def body(cols, carry):
            for far, target in ((0, mean), (1, sent)):
                parts = [landing(route, chunk, 2 * source + far, 1, top)[:, cols].astype(F32) for source in range(4)]
                target[route, chunk, :, cols] = (parts[0] + parts[1]) + (parts[2] + parts[3])
            return carry

        strips(body)

    def first_sums(chunk, carry, top):
        add_four(0, chunk, top)

        @pl.when(chunk > 0)
        def _():
            second(1, chunk - 1)

        add_four(1, chunk, top)
        second(0, chunk)
        return carry

    sweep(first_sums)
    second(1, N_CHUNK - 1)

    def finish(chunk, squares, top):
        for route in range(2):
            drain(got.at[route, chunk], second_recv.at[route, chunk])

            def body(cols, total):
                value = (mean[route, chunk, :, cols] + got[route, chunk, :, cols]) * 0.125
                mean[route, chunk, :, cols] = value
                return fold(total, value * value)

            squares = strips(body, squares)
            load(2, two_in, two, route, chunk, top)
            drain(sent.at[route, chunk], second_send.at[route, chunk])
            load(0, master_in, master, route, chunk, top)
        return squares

    def share_all(box, send_sem, recv_sem):
        for device in others():
            pltpu.make_async_remote_copy(src_ref=box.at[mine], dst_ref=box.at[mine], send_sem=send_sem, recv_sem=recv_sem, device_id=device, device_id_type=MESH).start()
        drain(box.at[pl.ds(0, 15)], recv_sem)

    total_box[mine] = sweep(finish, jnp.zeros((8, 128), F32))
    share_all(total_box, box_sem.at[0], box_sem.at[1])
    total = jnp.sum(jnp.sum(total_box[...], axis=0), keepdims=True)
    clip = jnp.minimum(1.0, MAX_NORM / jnp.sqrt(total))

    def update(route, chunk, carry):
        for which, block in enumerate((master, one, two)):
            drain(block.at[route, chunk], load_sem.at[which, route, chunk])

        def body(cols, carry):
            place = (route, chunk, slice(None), cols)
            weight = master[place]
            scaled = clip * mean[place]
            new_one = BETA_ONE * one[place] + (1.0 - BETA_ONE) * scaled
            new_two = BETA_TWO * two[place] + (1.0 - BETA_TWO) * scaled * scaled
            direction = (new_one * (1.0 / CORR_ONE)) / (jnp.sqrt(new_two * (1.0 / CORR_TWO)) + EPSILON) + WEIGHT_DECAY * weight
            one[place] = new_one
            two[place] = new_two
            mean[place] = direction
            return fold(carry[0], weight * weight), fold(carry[1], direction * direction)

        return strips(body, carry)

    for index, (low, high) in enumerate(((0, N_TOP), (N_TOP, N_CHUNK))):
        zero = jnp.zeros((8, 128), F32)
        weight_sq, direction_sq = lax.fori_loop(low, high, lambda chunk, carry: update(1, chunk, update(0, chunk, carry)), (zero, zero))
        norm_box[mine, index] = weight_sq
        norm_box[mine, 2 + index] = direction_sq
    share_all(norm_box, box_sem.at[2], box_sem.at[3])
    sums = jnp.sum(jnp.sum(norm_box[...], axis=0), axis=2, keepdims=True)
    row = lax.broadcasted_iota(jnp.int32, (8, 1), 0)

    def norms(top_rows, bot_rows):
        pieces = [jnp.sum(jnp.where(mask, top_rows, 0.0), axis=0, keepdims=True) for mask in (row < 3, row == 3, row > 3)]
        top_all = jnp.where(row < 3, pieces[0], jnp.where(row == 3, pieces[1], pieces[2]))
        return jnp.sqrt(top_all), jnp.sqrt(jnp.sum(bot_rows, axis=0, keepdims=True) + jnp.zeros_like(top_all))

    weight_norms, direction_norms = norms(sums[0], sums[1]), norms(sums[2], sums[3])
    bot_rate, top_rate = [LEARN_RATE * (weight_norms[index] / direction_norms[index]) for index in (1, 0)]

    def piece(place, route, chunk, top):
        if top:
            start = place * SHARD + route * TOP_ROUTE + chunk * COLS
        else:
            start = place * (SHARD // 2) + route * BOT_ROUTE + (chunk - N_TOP) * COLS
        return (top_out if top else bot_out).at[:, pl.ds(pl.multiple_of(start, COLS), COLS)]

    def part(place, top, share=1):
        size = SHARD if top else SHARD // 2
        return (top_out if top else bot_out).at[:, pl.ds(pl.multiple_of(place * size, size), size // share)]

    def weights(route, chunk, top):
        rate = top_rate if top else bot_rate
        view = piece(places[0], route, chunk, top)

        def body(cols, carry):
            place = (route, chunk, slice(None), cols)
            value = master[place] - rate * mean[place]
            master[place] = value
            view[:, cols] = value.astype(BF16)
            return carry

        strips(body)

    def send(route, chunk, top):
        view = piece(places[0], route, chunk, top)
        kind = int(top)
        for axis in range(2):
            copy_to(view, view, places[1 + axis], side_send.at[axis, kind], side_recv.at[axis, route, chunk])
        copy_to(view, view, partner, partner_send.at[0, kind], partner_recv.at[0, kind])

    def own(chunk, carry, top):
        weights(0, chunk, top)

        @pl.when(chunk > (0 if top else N_TOP))
        def _():
            send(1, chunk - 1, top)

        weights(1, chunk, top)
        send(0, chunk, top)

        @pl.when(chunk == (N_TOP - 1 if top else N_CHUNK - 1))
        def _():
            send(1, chunk, top)

        return carry

    def hand_on(chunk, carry, top):
        kind = int(top)
        for route in range(2):
            for axis in range(2):
                view = piece(places[1 + axis], route, chunk, top)
                drain(view, side_recv.at[axis, route, chunk])
                if axis == route:
                    copy_to(view, view, places[2 - axis], forward_send.at[route, kind], corner_recv.at[route, chunk])
                copy_to(view, view, partner, partner_send.at[1 + axis, kind], partner_recv.at[1 + axis, kind])
        return carry

    def corner(chunk, carry, top):
        for route in range(2):
            view = piece(places[3], route, chunk, top)
            drain(view, corner_recv.at[route, chunk])
            copy_to(view, view, partner, partner_send.at[3, int(top)], partner_recv.at[3, int(top)])
        return carry

    sweep(own)
    sweep(hand_on)
    sweep(corner)

    for top in (True, False):
        kind = int(top)
        for axis in range(2):
            drain(part(places[0], top), side_send.at[axis, kind])
            drain(part(places[0], top, 2), forward_send.at[axis, kind])
        for chip, (row_pos, col_pos) in enumerate(chips):
            drain(part(places[chip], top), partner_send.at[chip, kind])
            drain(part(data_index(row_pos, col_pos, flip(core)), top), partner_recv.at[chip, kind])
    drain(total_box.at[pl.ds(0, 15)], box_sem.at[0])
    drain(norm_box.at[pl.ds(0, 15)], box_sem.at[2])

    def first_sent(chunk, carry, top):
        for route in range(2):
            drain(landing(route, chunk, 2, 6, top), first_send.at[route, chunk])
        return carry

    sweep(first_sent)


def in_hbm(array):
    return pltpu.with_memory_space_constraint(array, pltpu.HBM)


def run_step(local_grads, master, moment_one, moment_two):
    dma = pltpu.SemaphoreType.DMA
    block = pltpu.VMEM((2, N_CHUNK, 8, COLS), F32)
    each = dma((2, N_CHUNK))
    return pl.pallas_call(
        step_kernel,
        out_shape=(pltpu.VMEM((8, 8 * SHARD), BF16), pltpu.VMEM((8, 4 * SHARD), BF16), block, block, block),
        in_specs=[pl.BlockSpec(memory_space=pltpu.HBM)] * 4,
        out_specs=(pl.BlockSpec(memory_space=pltpu.VMEM),) * 5,
        scratch_shapes=[
            block,
            pltpu.VMEM((16, 8, 128), F32),
            pltpu.VMEM((16, 4, 8, 128), F32),
            each, each, each, each, dma((3, 2, N_CHUNK)),
            dma((2, 2)), dma((2, 2, N_CHUNK)), dma((2, 2)), each, dma((4, 2)), dma((4, 2)), dma((4,)),
        ],
        compiler_params=pltpu.CompilerParams(collective_id=0, has_side_effects=True, vmem_limit_bytes=STEP_LIMIT),
        name='lamb_step',
    )(in_hbm(local_grads), in_hbm(master), in_hbm(moment_one), in_hbm(moment_two))


def write_kernel(top, bot, master, one, two, params_out, master_out, one_out, two_out, sem):
    copies = []
    for place in range(8):
        copies.append((top.at[:, pl.ds(place * SHARD, SHARD)], params_out.at[pl.ds(0, 8), pl.ds(place * SHARD, SHARD)]))
        for half in range(2):
            copies.append((bot.at[pl.ds(4 * half, 4), pl.ds(place * TOP_ROUTE, TOP_ROUTE)], params_out.at[pl.ds(8, 4), pl.ds(place * SHARD + half * TOP_ROUTE, TOP_ROUTE)]))
    for block, array in ((master, master_out), (one, one_out), (two, two_out)):
        for route in range(2):
            for chunk in range(N_CHUNK):
                copies += [(src, dst) for dst, src in row_views(array, 0, route, chunk, block.at[route, chunk], chunk < N_TOP)]
    for index, (src, dst) in enumerate(copies):
        pltpu.make_async_copy(src, dst, sem.at[index]).start()
    for index, (src, dst) in enumerate(copies):
        pltpu.make_async_copy(src, dst, sem.at[index]).wait()


def write_out(*blocks):
    state = jax.ShapeDtypeStruct((12, SHARD), F32)
    return pl.pallas_call(
        write_kernel,
        out_shape=(jax.ShapeDtypeStruct((12, 8 * SHARD), BF16), state, state, state),
        in_specs=[pl.BlockSpec(memory_space=pltpu.VMEM)] * 5,
        out_specs=(pl.BlockSpec(memory_space=pltpu.HBM),) * 4,
        scratch_shapes=[pltpu.SemaphoreType.DMA((24 + 6 * (N_TOP + 2 * N_BOT),))],
        compiler_params=pltpu.CompilerParams(vmem_limit_bytes=WRITE_LIMIT),
        name='write_out',
    )(*[pltpu.with_memory_space_constraint(block, pltpu.VMEM) for block in blocks])


def solution(mesh):
    state_spec = P(None, ('model', 'data'))

    def device_step(local_grads, master, moment_one, moment_two):
        return write_out(*run_step(local_grads, master, moment_one, moment_two))

    return jax.shard_map(device_step, mesh=mesh, in_specs=(P('data', None, 'model'), state_spec, state_spec, state_spec), out_specs=(P(None, 'model'), state_spec, state_spec, state_spec), check_vma=False)
```

time: 849 us -> 395 us (0.47)
  blocking collectives: 487 us -> 0 us
  Pallas kernels: 0 us -> 394 us
  waiting for transfers between devices: 176 us -> 0 us
  local copies, waits for them, and re-layouts: 108 us -> 0 us
  other arithmetic: 62.5 us -> 0 us
  between operations: 14.8 us -> 0.64 us
    all_to_all x1 -> x0, blocking collectives: 421 us -> none  [device_step(): received = lax.all_to_all(grad_slab, 'data', 1, 0, tiled=True)]
    pallas_call x0 -> x2, Pallas kernels: none -> 394 us  [the longest x1 377 us: run_step(): pl.pallas_call(step_kernel, out_shape=(pltpu.VMEM((8, 8 * SHARD), BF16),...]
    all_gather x1 -> x0, waiting for transfers between devices: 176 us -> none  [device_step(): lax.all_gather(new_master.astype(jnp.bfloat16), 'data', axis=1, tiled=True)]
    psum x2 -> x0, blocking collectives: 65.6 us -> none  [the longest x1 32.9 us: device_step(): lax.psum(jnp.stack([jnp.sum(master * master, axis=1), jnp.sum(direction *...]
    unnamed x2 -> x0, local copies, waits for them, and re-layouts: 58 us -> none
    all_to_all x2 -> x0, local copies, waits for them, and re-layouts: 46.9 us -> none  [device_step(): received = lax.all_to_all(grad_slab, 'data', 1, 0, tiled=True)]
    reduce_sum x5 -> x0, other arithmetic: 45 us -> none  [the longest x1 22.3 us: device_step(): jnp.sum(master * master, axis=1)]
    convert_element_type x1 -> x0, other arithmetic: 16.7 us -> none  [device_step(): new_master.astype(jnp.bfloat16)]
  transfers between devices with their start and end apart: 1 -> 0, of which waited for: 1 -> 0; matrix products, arithmetic and copies ran while one was open for 0% -> 0% of each run, Pallas kernels for 0% -> 0%
where the time goes in v2:
time: 395 us
  Pallas kernels  394 us (100%)
    pallas_call x1, Pallas kernels, run_step(): pl.pallas_call(step_kernel, out_shape=(pltpu.VMEM((8, 8 * SHARD), BF16),...  377 us
    pallas_call x1, Pallas kernels, write_out(): pl.pallas_call(write_kernel, out_shape=(jax.ShapeDtypeStruct((12, 8 * SHA...  16.5 us

profile of v2, /device:TPU:0, one launch (start us, length us, event | category | flops | bytes accessed | tf_op | source)
XLA Modules:
  0.0 394.6 jit_solution(4294107001731575406)
XLA Ops:
  0.6 377.5 %lamb_step.1 = (bf16[8,1179648]{1,0:T(8,128)(2,1)S(1)}, bf16[8,589824]{1,0:T(8,128)(2,1)S(1)}, f32[2,9,8,12288]{3,2,1,0:T(8,128)S(1)}, f32[2,9,8,12288]{3,2,1,0:T(8,128)S(1)}, f32[2,9,8,12288]{3,2,1,0:T(8,128)S(1)}) custom-call(bf16[1,12,1179648]{2,1,0:T(8,128)(2,1)} %grads.1, f32[12,147456]{1,0:T(8,128)} %master_in.1, f32[12,147456]{1,0:T(8,128)} %one_in.1, ...), custom_call_target="tpu_custom_call" | custom-call | tf_op jit(solution)/shard_map/lamb_step/pallas_call | solution.py:349
  378.1 16.5 %write_out.1 = (bf16[12,1179648]{1,0:T(8,128)(2,1)}, f32[12,147456]{1,0:T(8,128)}, f32[12,147456]{1,0:T(8,128)}, f32[12,147456]{1,0:T(8,128)}) custom-call(bf16[8,1179648]{1,0:T(8,128)(2,1)S(1)} %get-tuple-element.9.top, bf16[8,589824]{1,0:T(8,128)(2,1)S(1)} %get-tuple-element.10.bot, f32[2,9,8,12288]{3,2,1,0:T(8,128)S(1)} %get-tuple-element.11.master, ...), custom_call_target="tpu_custom_call" | custom-call | tf_op jit(solution)/shard_map/write_out/pallas_call | solution.py:384

commit v3 on v2

--- a/solution.py
+++ b/solution.py
@@ -28,8 +28,9 @@
 N_TOP = TOP_ROUTE // COLS
 N_BOT = BOT_ROUTE // COLS
 N_CHUNK = N_TOP + N_BOT
-STRIP = 512
-
+STRIP = 1024
+
+TINY = 1.2e-38
 MIB = 1024 * 1024
 STEP_LIMIT = 9 * MIB
 WRITE_LIMIT = STEP_LIMIT
@@ -208,12 +209,13 @@
     def share_all(box, send_sem, recv_sem):
         for device in others():
             pltpu.make_async_remote_copy(src_ref=box.at[mine], dst_ref=box.at[mine], send_sem=send_sem, recv_sem=recv_sem, device_id=device, device_id_type=MESH).start()
-        drain(box.at[pl.ds(0, 15)], recv_sem)
 
     total_box[mine] = sweep(finish, jnp.zeros((8, 128), F32))
     share_all(total_box, box_sem.at[0], box_sem.at[1])
+    drain(total_box.at[pl.ds(0, 15)], box_sem.at[1])
     total = jnp.sum(jnp.sum(total_box[...], axis=0), keepdims=True)
     clip = jnp.minimum(1.0, MAX_NORM / jnp.sqrt(total))
+    one_scale, two_scale = clip * (1.0 - BETA_ONE), clip * (1.0 - BETA_TWO) ** 0.5
 
     def update(route, chunk, carry):
         for which, block in enumerate((master, one, two)):
@@ -222,33 +224,49 @@
         def body(cols, carry):
             place = (route, chunk, slice(None), cols)
             weight = master[place]
-            scaled = clip * mean[place]
-            new_one = BETA_ONE * one[place] + (1.0 - BETA_ONE) * scaled
-            new_two = BETA_TWO * two[place] + (1.0 - BETA_TWO) * scaled * scaled
-            direction = (new_one * (1.0 / CORR_ONE)) / (jnp.sqrt(new_two * (1.0 / CORR_TWO)) + EPSILON) + WEIGHT_DECAY * weight
+            value = mean[place]
+            new_one = BETA_ONE * one[place] + one_scale * value
+            change = two_scale * value
+            new_two = BETA_TWO * two[place] + change * change
             one[place] = new_one
             two[place] = new_two
+            floor = jnp.maximum(new_two, TINY)
+            root = floor * lax.rsqrt(floor)
+            direction = (new_one * (CORR_TWO ** 0.5 / CORR_ONE)) / (root + EPSILON * CORR_TWO ** 0.5) + WEIGHT_DECAY * weight
             mean[place] = direction
             return fold(carry[0], weight * weight), fold(carry[1], direction * direction)
 
         return strips(body, carry)
 
-    for index, (low, high) in enumerate(((0, N_TOP), (N_TOP, N_CHUNK))):
+    def update_rows(index, low, high):
         zero = jnp.zeros((8, 128), F32)
         weight_sq, direction_sq = lax.fori_loop(low, high, lambda chunk, carry: update(1, chunk, update(0, chunk, carry)), (zero, zero))
-        norm_box[mine, index] = weight_sq
-        norm_box[mine, 2 + index] = direction_sq
-    share_all(norm_box, box_sem.at[2], box_sem.at[3])
-    sums = jnp.sum(jnp.sum(norm_box[...], axis=0), axis=2, keepdims=True)
-    row = lax.broadcasted_iota(jnp.int32, (8, 1), 0)
-
-    def norms(top_rows, bot_rows):
-        pieces = [jnp.sum(jnp.where(mask, top_rows, 0.0), axis=0, keepdims=True) for mask in (row < 3, row == 3, row > 3)]
-        top_all = jnp.where(row < 3, pieces[0], jnp.where(row == 3, pieces[1], pieces[2]))
-        return jnp.sqrt(top_all), jnp.sqrt(jnp.sum(bot_rows, axis=0, keepdims=True) + jnp.zeros_like(top_all))
-
-    weight_norms, direction_norms = norms(sums[0], sums[1]), norms(sums[2], sums[3])
-    bot_rate, top_rate = [LEARN_RATE * (weight_norms[index] / direction_norms[index]) for index in (1, 0)]
+        box = norm_box.at[index]
+        box[mine, 0] = weight_sq
+        box[mine, 1] = direction_sq
+        share_all(box, box_sem.at[2 + index], box_sem.at[4 + index])
+
+    def row_sums(index):
+        box = norm_box.at[index]
+        drain(box.at[pl.ds(0, 15)], box_sem.at[4 + index])
+        return jnp.sum(jnp.sum(box[...], axis=0), axis=2, keepdims=True)
+
+    def bot_rate():
+        sums = jnp.sqrt(jnp.sum(row_sums(0), axis=1, keepdims=True))
+        return LEARN_RATE * (sums[0] / sums[1]) + jnp.zeros((8, 1), F32)
+
+    def top_rate():
+        sums = row_sums(1)
+        row = lax.broadcasted_iota(jnp.int32, (8, 1), 0)
+
+        def norms(values):
+            pieces = [jnp.sum(jnp.where(mask, values, 0.0), axis=0, keepdims=True) for mask in (row < 3, row == 3, row > 3)]
+            return jnp.sqrt(jnp.where(row < 3, pieces[0], jnp.where(row == 3, pieces[1], pieces[2])))
+
+        return LEARN_RATE * (norms(sums[0]) / norms(sums[1]))
+
+    update_rows(0, N_TOP, N_CHUNK)
+    update_rows(1, 0, N_TOP)
 
     def piece(place, route, chunk, top):
         if top:
@@ -261,8 +279,7 @@
         size = SHARD if top else SHARD // 2
         return (top_out if top else bot_out).at[:, pl.ds(pl.multiple_of(place * size, size), size // share)]
 
-    def weights(route, chunk, top):
-        rate = top_rate if top else bot_rate
+    def weights(route, chunk, rate, top):
         view = piece(places[0], route, chunk, top)
 
         def body(cols, carry):
@@ -281,21 +298,21 @@
             copy_to(view, view, places[1 + axis], side_send.at[axis, kind], side_recv.at[axis, route, chunk])
         copy_to(view, view, partner, partner_send.at[0, kind], partner_recv.at[0, kind])
 
-    def own(chunk, carry, top):
-        weights(0, chunk, top)
+    def own(chunk, rate, top):
+        weights(0, chunk, rate, top)
 
         @pl.when(chunk > (0 if top else N_TOP))
         def _():
             send(1, chunk - 1, top)
 
-        weights(1, chunk, top)
+        weights(1, chunk, rate, top)
         send(0, chunk, top)
 
         @pl.when(chunk == (N_TOP - 1 if top else N_CHUNK - 1))
         def _():
             send(1, chunk, top)
 
-        return carry
+        return rate
 
     def hand_on(chunk, carry, top):
         kind = int(top)
@@ -315,9 +332,14 @@
             copy_to(view, view, partner, partner_send.at[3, int(top)], partner_recv.at[3, int(top)])
         return carry
 
-    sweep(own)
-    sweep(hand_on)
-    sweep(corner)
+    def bottom_first(body, carry=0):
+        carry = lax.fori_loop(N_TOP, N_CHUNK, functools.partial(body, top=False), carry)
+        return lax.fori_loop(0, N_TOP, functools.partial(body, top=True), carry)
+
+    lax.fori_loop(N_TOP, N_CHUNK, functools.partial(own, top=False), bot_rate())
+    lax.fori_loop(0, N_TOP, functools.partial(own, top=True), top_rate())
+    bottom_first(hand_on)
+    bottom_first(corner)
 
     for top in (True, False):
         kind = int(top)
@@ -328,7 +350,8 @@
             drain(part(places[chip], top), partner_send.at[chip, kind])
             drain(part(data_index(row_pos, col_pos, flip(core)), top), partner_recv.at[chip, kind])
     drain(total_box.at[pl.ds(0, 15)], box_sem.at[0])
-    drain(norm_box.at[pl.ds(0, 15)], box_sem.at[2])
+    for index in range(2):
+        drain(norm_box.at[index, pl.ds(0, 15)], box_sem.at[2 + index])
 
     def first_sent(chunk, carry, top):
         for route in range(2):
@@ -354,9 +377,9 @@
         scratch_shapes=[
             block,
             pltpu.VMEM((16, 8, 128), F32),
-            pltpu.VMEM((16, 4, 8, 128), F32),
+            pltpu.VMEM((2, 16, 2, 8, 128), F32),
             each, each, each, each, dma((3, 2, N_CHUNK)),
-            dma((2, 2)), dma((2, 2, N_CHUNK)), dma((2, 2)), each, dma((4, 2)), dma((4, 2)), dma((4,)),
+            dma((2, 2)), dma((2, 2, N_CHUNK)), dma((2, 2)), each, dma((4, 2)), dma((4, 2)), dma((6,)),
         ],
         compiler_params=pltpu.CompilerParams(collective_id=0, has_side_effects=True, vmem_limit_bytes=STEP_LIMIT),
         name='lamb_step',

time: 395 us -> 384 us (0.972)
  Pallas kernels: 394 us -> 383 us
    pallas_call x1, Pallas kernels: 377 us -> 367 us  [run_step(): pl.pallas_call(step_kernel, out_shape=(pltpu.VMEM((8, 8 * SHARD), BF16),...]
where the time goes in v3:
time: 384 us
  Pallas kernels  383 us (100%)
    pallas_call x1, Pallas kernels, run_step(): pl.pallas_call(step_kernel, out_shape=(pltpu.VMEM((8, 8 * SHARD), BF16),...  367 us
    pallas_call x1, Pallas kernels, write_out(): pl.pallas_call(write_kernel, out_shape=(jax.ShapeDtypeStruct((12, 8 * SHA...  16.5 us

profile of v3, /device:TPU:0, one launch (start us, length us, event | category | flops | bytes accessed | tf_op | source)
XLA Modules:
  0.0 384.0 jit_solution(13037952780942174561)
XLA Ops:
  0.6 366.8 %lamb_step.1 = (bf16[8,1179648]{1,0:T(8,128)(2,1)S(1)}, bf16[8,589824]{1,0:T(8,128)(2,1)S(1)}, f32[2,9,8,12288]{3,2,1,0:T(8,128)S(1)}, f32[2,9,8,12288]{3,2,1,0:T(8,128)S(1)}, f32[2,9,8,12288]{3,2,1,0:T(8,128)S(1)}) custom-call(bf16[1,12,1179648]{2,1,0:T(8,128)(2,1)} %grads.1, f32[12,147456]{1,0:T(8,128)} %master_in.1, f32[12,147456]{1,0:T(8,128)} %one_in.1, ...), custom_call_target="tpu_custom_call" | custom-call | tf_op jit(solution)/shard_map/lamb_step/pallas_call | solution.py:372
  367.4 16.5 %write_out.1 = (bf16[12,1179648]{1,0:T(8,128)(2,1)}, f32[12,147456]{1,0:T(8,128)}, f32[12,147456]{1,0:T(8,128)}, f32[12,147456]{1,0:T(8,128)}) custom-call(bf16[8,1179648]{1,0:T(8,128)(2,1)S(1)} %get-tuple-element.9.top, bf16[8,589824]{1,0:T(8,128)(2,1)S(1)} %get-tuple-element.10.bot, f32[2,9,8,12288]{3,2,1,0:T(8,128)S(1)} %get-tuple-element.11.master, ...), custom_call_target="tpu_custom_call" | custom-call | tf_op jit(solution)/shard_map/write_out/pallas_call | solution.py:407

commit v4 on v3

--- a/solution.py
+++ b/solution.py
@@ -28,7 +28,9 @@
 N_TOP = TOP_ROUTE // COLS
 N_BOT = BOT_ROUTE // COLS
 N_CHUNK = N_TOP + N_BOT
+N_EARLY = 2 * N_TOP // 3
 STRIP = 1024
+UPDATE_STRIP = 2048
 
 TINY = 1.2e-38
 MIB = 1024 * 1024
@@ -54,13 +56,6 @@
     for step in range(1, 16):
         other = lax.rem(mine + step, 16)
         yield other // 8, lax.rem(other, 8)
-
-
-def enter_all():
-    barrier = pltpu.get_barrier_semaphore()
-    for device in others():
-        pl.semaphore_signal(barrier, inc=1, device_id=device, device_id_type=MESH)
-    pl.semaphore_wait(barrier, 15)
 
 
 def drain(ref, sem):
@@ -83,15 +78,15 @@
     return lax.fori_loop(N_TOP, N_CHUNK, functools.partial(body, top=False), carry)
 
 
-def strips(body, carry=0):
+def strips(body, carry=0, width=STRIP):
     def step(strip, carry):
-        return body(pl.ds(pl.multiple_of(strip * STRIP, STRIP), STRIP), carry)
-
-    return lax.fori_loop(0, COLS // STRIP, step, carry)
+        return body(pl.ds(pl.multiple_of(strip * width, width), width), carry)
+
+    return lax.fori_loop(0, COLS // width, step, carry)
 
 
 def fold(total, values):
-    for tile in range(STRIP // 128):
+    for tile in range(values.shape[1] // 128):
         total = total + values[:, tile * 128:(tile + 1) * 128]
     return total
 
@@ -101,7 +96,7 @@
     top_out, bot_out, master, one, two,
     mean, total_box, norm_box,
     first_send, first_recv, second_send, second_recv, load_sem,
-    side_send, side_recv, forward_send, corner_recv, partner_send, partner_recv, box_sem,
+    side_send, side_recv, forward_send, corner_recv, partner_send, partner_recv, box_sem, seen, known,
 ):
     pos_y, pos_x, core = my_place()
     model_pos = lax.axis_index('model')
@@ -152,9 +147,18 @@
         for src, dst in row_views(array, 0, route, chunk, block.at[route, chunk], top):
             pltpu.make_async_copy(src, dst, load_sem.at[which, route, chunk]).start()
 
+    next_to = [(model_pos, place) for chip in (1, 2) for place in (places[chip], data_index(*chips[chip], flip(core)))] + [(model_pos, partner), (flip(model_pos), places[0])]
+
+    def tell(sem, devices):
+        for device in devices:
+            pl.semaphore_signal(sem, inc=1, device_id=device, device_id_type=MESH)
+
     sweep(local)
-    enter_all()
+    barrier = pltpu.get_barrier_semaphore()
+    tell(barrier, next_to)
+    pl.semaphore_wait(barrier, len(next_to))
     sweep(remote)
+    tell(seen, next_to)
 
     def load_one(chunk, carry, top):
         for route in range(2):
@@ -162,6 +166,8 @@
         return carry
 
     sweep(load_one)
+    pl.semaphore_wait(seen, len(next_to))
+    tell(known, next_to[-1:])
 
     def second(route, chunk):
         copy_to(sent.at[route, chunk], got.at[route, chunk], places[2 - route], second_send.at[route, chunk], second_recv.at[route, chunk])
@@ -211,6 +217,7 @@
             pltpu.make_async_remote_copy(src_ref=box.at[mine], dst_ref=box.at[mine], send_sem=send_sem, recv_sem=recv_sem, device_id=device, device_id_type=MESH).start()
 
     total_box[mine] = sweep(finish, jnp.zeros((8, 128), F32))
+    pl.semaphore_wait(known, 1)
     share_all(total_box, box_sem.at[0], box_sem.at[1])
     drain(total_box.at[pl.ds(0, 15)], box_sem.at[1])
     total = jnp.sum(jnp.sum(total_box[...], axis=0), keepdims=True)
@@ -236,14 +243,15 @@
             mean[place] = direction
             return fold(carry[0], weight * weight), fold(carry[1], direction * direction)
 
-        return strips(body, carry)
-
-    def update_rows(index, low, high):
+        return strips(body, carry, UPDATE_STRIP)
+
+    def update_rows(low, high, carry=None):
         zero = jnp.zeros((8, 128), F32)
-        weight_sq, direction_sq = lax.fori_loop(low, high, lambda chunk, carry: update(1, chunk, update(0, chunk, carry)), (zero, zero))
+        return lax.fori_loop(low, high, lambda chunk, carry: update(1, chunk, update(0, chunk, carry)), carry or (zero, zero))
+
+    def share_norms(index, squares):
         box = norm_box.at[index]
-        box[mine, 0] = weight_sq
-        box[mine, 1] = direction_sq
+        box[mine, 0], box[mine, 1] = squares
         share_all(box, box_sem.at[2 + index], box_sem.at[4 + index])
 
     def row_sums(index):
@@ -265,8 +273,8 @@
 
         return LEARN_RATE * (norms(sums[0]) / norms(sums[1]))
 
-    update_rows(0, N_TOP, N_CHUNK)
-    update_rows(1, 0, N_TOP)
+    share_norms(0, update_rows(N_TOP, N_CHUNK))
+    top_squares = update_rows(0, N_EARLY)
 
     def piece(place, route, chunk, top):
         if top:
@@ -337,6 +345,7 @@
         return lax.fori_loop(0, N_TOP, functools.partial(body, top=True), carry)
 
     lax.fori_loop(N_TOP, N_CHUNK, functools.partial(own, top=False), bot_rate())
+    share_norms(1, update_rows(N_EARLY, N_TOP, top_squares))
     lax.fori_loop(0, N_TOP, functools.partial(own, top=True), top_rate())
     bottom_first(hand_on)
     bottom_first(corner)
@@ -380,6 +389,7 @@
             pltpu.VMEM((2, 16, 2, 8, 128), F32),
             each, each, each, each, dma((3, 2, N_CHUNK)),
             dma((2, 2)), dma((2, 2, N_CHUNK)), dma((2, 2)), each, dma((4, 2)), dma((4, 2)), dma((6,)),
+            pltpu.SemaphoreType.REGULAR, pltpu.SemaphoreType.REGULAR,
         ],
         compiler_params=pltpu.CompilerParams(collective_id=0, has_side_effects=True, vmem_limit_bytes=STEP_LIMIT),
         name='lamb_step',

time: 384 us -> 385 us (level)
  no operation moved by 1% of the time
where the time goes in v4:
time: 385 us
  Pallas kernels  384 us (100%)
    pallas_call x1, Pallas kernels, run_step(): pl.pallas_call(step_kernel, out_shape=(pltpu.VMEM((8, 8 * SHARD), BF16),...  368 us
    pallas_call x1, Pallas kernels, write_out(): pl.pallas_call(write_kernel, out_shape=(jax.ShapeDtypeStruct((12, 8 * SHA...  16.5 us

profile of v4, /device:TPU:0, one launch (start us, length us, event | category | flops | bytes accessed | tf_op | source)
XLA Modules:
  0.0 384.7 jit_solution(6486385907544676484)
XLA Ops:
  0.6 367.5 %lamb_step.1 = (bf16[8,1179648]{1,0:T(8,128)(2,1)S(1)}, bf16[8,589824]{1,0:T(8,128)(2,1)S(1)}, f32[2,9,8,12288]{3,2,1,0:T(8,128)S(1)}, f32[2,9,8,12288]{3,2,1,0:T(8,128)S(1)}, f32[2,9,8,12288]{3,2,1,0:T(8,128)S(1)}) custom-call(bf16[1,12,1179648]{2,1,0:T(8,128)(2,1)} %grads.1, f32[12,147456]{1,0:T(8,128)} %master_in.1, f32[12,147456]{1,0:T(8,128)} %one_in.1, ...), custom_call_target="tpu_custom_call" | custom-call | tf_op jit(solution)/shard_map/lamb_step/pallas_call | solution.py:381
  368.1 16.5 %write_out.1 = (bf16[12,1179648]{1,0:T(8,128)(2,1)}, f32[12,147456]{1,0:T(8,128)}, f32[12,147456]{1,0:T(8,128)}, f32[12,147456]{1,0:T(8,128)}) custom-call(bf16[8,1179648]{1,0:T(8,128)(2,1)S(1)} %get-tuple-element.9.top, bf16[8,589824]{1,0:T(8,128)(2,1)S(1)} %get-tuple-element.10.bot, f32[2,9,8,12288]{3,2,1,0:T(8,128)S(1)} %get-tuple-element.11.master, ...), custom_call_target="tpu_custom_call" | custom-call | tf_op jit(solution)/shard_map/write_out/pallas_call | solution.py:417

commit v5 on v4

--- a/solution.py
+++ b/solution.py
@@ -28,7 +28,6 @@
 N_TOP = TOP_ROUTE // COLS
 N_BOT = BOT_ROUTE // COLS
 N_CHUNK = N_TOP + N_BOT
-N_EARLY = 2 * N_TOP // 3
 STRIP = 1024
 UPDATE_STRIP = 2048
 
@@ -245,9 +244,9 @@
 
         return strips(body, carry, UPDATE_STRIP)
 
-    def update_rows(low, high, carry=None):
+    def update_rows(low, high):
         zero = jnp.zeros((8, 128), F32)
-        return lax.fori_loop(low, high, lambda chunk, carry: update(1, chunk, update(0, chunk, carry)), carry or (zero, zero))
+        return lax.fori_loop(low, high, lambda chunk, carry: update(1, chunk, update(0, chunk, carry)), (zero, zero))
 
     def share_norms(index, squares):
         box = norm_box.at[index]
@@ -274,7 +273,7 @@
         return LEARN_RATE * (norms(sums[0]) / norms(sums[1]))
 
     share_norms(0, update_rows(N_TOP, N_CHUNK))
-    top_squares = update_rows(0, N_EARLY)
+    share_norms(1, update_rows(0, N_TOP))
 
     def piece(place, route, chunk, top):
         if top:
@@ -345,7 +344,6 @@
         return lax.fori_loop(0, N_TOP, functools.partial(body, top=True), carry)
 
     lax.fori_loop(N_TOP, N_CHUNK, functools.partial(own, top=False), bot_rate())
-    share_norms(1, update_rows(N_EARLY, N_TOP, top_squares))
     lax.fori_loop(0, N_TOP, functools.partial(own, top=True), top_rate())
     bottom_first(hand_on)
     bottom_first(corner)

time: 385 us -> 381 us (0.990)
  no operation moved by 1% of the time
where the time goes in v5:
time: 381 us
  Pallas kernels  381 us (100%)
    pallas_call x1, Pallas kernels, run_step(): pl.pallas_call(step_kernel, out_shape=(pltpu.VMEM((8, 8 * SHARD), BF16),...  364 us
    pallas_call x1, Pallas kernels, write_out(): pl.pallas_call(write_kernel, out_shape=(jax.ShapeDtypeStruct((12, 8 * SHA...  16.5 us

profile of v5, /device:TPU:0, one launch (start us, length us, event | category | flops | bytes accessed | tf_op | source)
XLA Modules:
  0.0 381.3 jit_solution(17466701001340912070)
XLA Ops:
  0.6 364.1 %lamb_step.1 = (bf16[8,1179648]{1,0:T(8,128)(2,1)S(1)}, bf16[8,589824]{1,0:T(8,128)(2,1)S(1)}, f32[2,9,8,12288]{3,2,1,0:T(8,128)S(1)}, f32[2,9,8,12288]{3,2,1,0:T(8,128)S(1)}, f32[2,9,8,12288]{3,2,1,0:T(8,128)S(1)}) custom-call(bf16[1,12,1179648]{2,1,0:T(8,128)(2,1)} %grads.1, f32[12,147456]{1,0:T(8,128)} %master_in.1, f32[12,147456]{1,0:T(8,128)} %one_in.1, ...), custom_call_target="tpu_custom_call" | custom-call | tf_op jit(solution)/shard_map/lamb_step/pallas_call | solution.py:379
  364.8 16.5 %write_out.1 = (bf16[12,1179648]{1,0:T(8,128)(2,1)}, f32[12,147456]{1,0:T(8,128)}, f32[12,147456]{1,0:T(8,128)}, f32[12,147456]{1,0:T(8,128)}) custom-call(bf16[8,1179648]{1,0:T(8,128)(2,1)S(1)} %get-tuple-element.9.top, bf16[8,589824]{1,0:T(8,128)(2,1)S(1)} %get-tuple-element.10.bot, f32[2,9,8,12288]{3,2,1,0:T(8,128)S(1)} %get-tuple-element.11.master, ...), custom_call_target="tpu_custom_call" | custom-call | tf_op jit(solution)/shard_map/write_out/pallas_call | solution.py:415

commit v6 on v5

--- a/solution.py
+++ b/solution.py
@@ -33,7 +33,7 @@
 
 TINY = 1.2e-38
 MIB = 1024 * 1024
-STEP_LIMIT = 9 * MIB
+STEP_LIMIT = 15 * MIB
 WRITE_LIMIT = STEP_LIMIT
 
 
@@ -93,15 +93,15 @@
 def step_kernel(
     grads, master_in, one_in, two_in,
     top_out, bot_out, master, one, two,
-    mean, total_box, norm_box,
-    first_send, first_recv, second_send, second_recv, load_sem,
-    side_send, side_recv, forward_send, corner_recv, partner_send, partner_recv, box_sem, seen, known,
+    mean, sent, total_box, norm_box,
+    near_recv, corner_recv, first_send, second_send, load_sem, side_send, forward_send, partner_send, partner_recv, box_sem, seen, known,
 ):
     pos_y, pos_x, core = my_place()
     model_pos = lax.axis_index('model')
     mine = model_pos * 8 + lax.axis_index('data')
     grad = grads.at[0]
-    sent, got = master, two
+    got = two
+    first_recv, second_recv = near_recv.at[0], near_recv.at[1]
     chips = ((pos_y, pos_x), (pos_y, flip(pos_x)), (flip(pos_y), pos_x), (flip(pos_y), flip(pos_x)))
     places = [data_index(row, col, core) for row, col in chips]
     partner = data_index(pos_y, pos_x, flip(core))
@@ -135,16 +135,16 @@
                     to_core = lax.rem(core + other, 2)
                     shard = data_index(*wanted(route, row, col, far), to_core)
                     for src, dst in row_views(grad, shard, route, chunk, landing(route, chunk, 4 + 2 * other + far, 1, top), top):
-                        copy_to(src, dst, data_index(row, col, to_core), first_send.at[route, chunk], first_recv.at[route, chunk])
+                        copy_to(src, dst, data_index(row, col, to_core), first_send.at[int(top)], first_recv.at[route, chunk])
             for route in range(2):
                 shard = data_index(*wanted(route, pos_y, pos_x, far), flip(core))
                 for src, dst in row_views(grad, shard, route, chunk, landing(route, chunk, 2 + far, 1, top), top):
-                    copy_to(src, dst, partner, first_send.at[route, chunk], first_recv.at[route, chunk])
+                    copy_to(src, dst, partner, first_send.at[int(top)], first_recv.at[route, chunk])
         return carry
 
-    def load(which, array, block, route, chunk, top):
+    def load(array, block, sem, route, chunk, top):
         for src, dst in row_views(array, 0, route, chunk, block.at[route, chunk], top):
-            pltpu.make_async_copy(src, dst, load_sem.at[which, route, chunk]).start()
+            pltpu.make_async_copy(src, dst, sem).start()
 
     next_to = [(model_pos, place) for chip in (1, 2) for place in (places[chip], data_index(*chips[chip], flip(core)))] + [(model_pos, partner), (flip(model_pos), places[0])]
 
@@ -152,48 +152,53 @@
         for device in devices:
             pl.semaphore_signal(sem, inc=1, device_id=device, device_id_type=MESH)
 
-    sweep(local)
     barrier = pltpu.get_barrier_semaphore()
     tell(barrier, next_to)
+    sweep(local)
     pl.semaphore_wait(barrier, len(next_to))
     sweep(remote)
     tell(seen, next_to)
 
-    def load_one(chunk, carry, top):
-        for route in range(2):
-            load(1, one_in, one, route, chunk, top)
+    def load_state(chunk, carry, top):
+        for route in range(2):
+            load(master_in, master, load_sem.at[0], route, chunk, top)
+            load(one_in, one, load_sem.at[1], route, chunk, top)
         return carry
 
-    sweep(load_one)
+    sweep(load_state)
     pl.semaphore_wait(seen, len(next_to))
     tell(known, next_to[-1:])
 
     def second(route, chunk):
-        copy_to(sent.at[route, chunk], got.at[route, chunk], places[2 - route], second_send.at[route, chunk], second_recv.at[route, chunk])
-
-    def add_four(route, chunk, top):
+        copy_to(sent.at[route, chunk], got.at[route, chunk], places[2 - route], second_send, second_recv.at[route, chunk])
+
+    def add_four(route, chunk, squares, top):
         drain(landing(route, chunk, 0, 8, top), first_recv.at[route, chunk])
 
-        def body(cols, carry):
+        def body(cols, total):
             for far, target in ((0, mean), (1, sent)):
                 parts = [landing(route, chunk, 2 * source + far, 1, top)[:, cols].astype(F32) for source in range(4)]
                 target[route, chunk, :, cols] = (parts[0] + parts[1]) + (parts[2] + parts[3])
-            return carry
-
-        strips(body)
-
-    def first_sums(chunk, carry, top):
-        add_four(0, chunk, top)
+            weight = master[route, chunk, :, cols]
+            return fold(total, weight * weight)
+
+        return strips(body, squares)
+
+    def first_sums(chunk, squares, top):
+        squares = add_four(0, chunk, squares, top)
 
         @pl.when(chunk > 0)
         def _():
             second(1, chunk - 1)
 
-        add_four(1, chunk, top)
+        squares = add_four(1, chunk, squares, top)
         second(0, chunk)
-        return carry
-
-    sweep(first_sums)
+        return squares
+
+    drain(master, load_sem.at[0])
+    zero = jnp.zeros((8, 128), F32)
+    top_squares = lax.fori_loop(0, N_TOP, functools.partial(first_sums, top=True), zero)
+    bot_squares = lax.fori_loop(N_TOP, N_CHUNK, functools.partial(first_sums, top=False), zero)
     second(1, N_CHUNK - 1)
 
     def finish(chunk, squares, top):
@@ -206,16 +211,14 @@
                 return fold(total, value * value)
 
             squares = strips(body, squares)
-            load(2, two_in, two, route, chunk, top)
-            drain(sent.at[route, chunk], second_send.at[route, chunk])
-            load(0, master_in, master, route, chunk, top)
+            load(two_in, two, load_sem.at[2 + int(top)], route, chunk, top)
         return squares
 
     def share_all(box, send_sem, recv_sem):
         for device in others():
             pltpu.make_async_remote_copy(src_ref=box.at[mine], dst_ref=box.at[mine], send_sem=send_sem, recv_sem=recv_sem, device_id=device, device_id_type=MESH).start()
 
-    total_box[mine] = sweep(finish, jnp.zeros((8, 128), F32))
+    total_box[mine] = sweep(finish, zero)
     pl.semaphore_wait(known, 1)
     share_all(total_box, box_sem.at[0], box_sem.at[1])
     drain(total_box.at[pl.ds(0, 15)], box_sem.at[1])
@@ -224,10 +227,7 @@
     one_scale, two_scale = clip * (1.0 - BETA_ONE), clip * (1.0 - BETA_TWO) ** 0.5
 
     def update(route, chunk, carry):
-        for which, block in enumerate((master, one, two)):
-            drain(block.at[route, chunk], load_sem.at[which, route, chunk])
-
-        def body(cols, carry):
+        def body(cols, total):
             place = (route, chunk, slice(None), cols)
             weight = master[place]
             value = mean[place]
@@ -240,17 +240,15 @@
             root = floor * lax.rsqrt(floor)
             direction = (new_one * (CORR_TWO ** 0.5 / CORR_ONE)) / (root + EPSILON * CORR_TWO ** 0.5) + WEIGHT_DECAY * weight
             mean[place] = direction
-            return fold(carry[0], weight * weight), fold(carry[1], direction * direction)
+            return fold(total, direction * direction)
 
         return strips(body, carry, UPDATE_STRIP)
 
-    def update_rows(low, high):
-        zero = jnp.zeros((8, 128), F32)
-        return lax.fori_loop(low, high, lambda chunk, carry: update(1, chunk, update(0, chunk, carry)), (zero, zero))
-
-    def share_norms(index, squares):
+    def update_rows(index, low, high, weight_squares):
+        drain(two.at[:, pl.ds(low, high - low)], load_sem.at[2 + index])
         box = norm_box.at[index]
-        box[mine, 0], box[mine, 1] = squares
+        box[mine, 0] = weight_squares
+        box[mine, 1] = lax.fori_loop(low, high, lambda chunk, total: update(1, chunk, update(0, chunk, total)), zero)
         share_all(box, box_sem.at[2 + index], box_sem.at[4 + index])
 
     def row_sums(index):
@@ -272,8 +270,9 @@
 
         return LEARN_RATE * (norms(sums[0]) / norms(sums[1]))
 
-    share_norms(0, update_rows(N_TOP, N_CHUNK))
-    share_norms(1, update_rows(0, N_TOP))
+    drain(one, load_sem.at[1])
+    update_rows(0, N_TOP, N_CHUNK, bot_squares)
+    update_rows(1, 0, N_TOP, top_squares)
 
     def piece(place, route, chunk, top):
         if top:
@@ -302,7 +301,7 @@
         view = piece(places[0], route, chunk, top)
         kind = int(top)
         for axis in range(2):
-            copy_to(view, view, places[1 + axis], side_send.at[axis, kind], side_recv.at[axis, route, chunk])
+            copy_to(view, view, places[1 + axis], side_send.at[axis, kind], near_recv.at[axis, route, chunk])
         copy_to(view, view, partner, partner_send.at[0, kind], partner_recv.at[0, kind])
 
     def own(chunk, rate, top):
@@ -326,7 +325,7 @@
         for route in range(2):
             for axis in range(2):
                 view = piece(places[1 + axis], route, chunk, top)
-                drain(view, side_recv.at[axis, route, chunk])
+                drain(view, near_recv.at[axis, route, chunk])
                 if axis == route:
                     copy_to(view, view, places[2 - axis], forward_send.at[route, kind], corner_recv.at[route, chunk])
                 copy_to(view, view, partner, partner_send.at[1 + axis, kind], partner_recv.at[1 + axis, kind])
@@ -360,12 +359,9 @@
     for index in range(2):
         drain(norm_box.at[index, pl.ds(0, 15)], box_sem.at[2 + index])
 
-    def first_sent(chunk, carry, top):
-        for route in range(2):
-            drain(landing(route, chunk, 2, 6, top), first_send.at[route, chunk])
-        return carry
-
-    sweep(first_sent)
+    drain(top_out.at[:, pl.ds(0, 6 * SHARD)], first_send.at[1])
+    drain(bot_out.at[:, pl.ds(0, 3 * SHARD)], first_send.at[0])
+    drain(sent, second_send)
 
 
 def in_hbm(array):
@@ -375,18 +371,16 @@
 def run_step(local_grads, master, moment_one, moment_two):
     dma = pltpu.SemaphoreType.DMA
     block = pltpu.VMEM((2, N_CHUNK, 8, COLS), F32)
-    each = dma((2, N_CHUNK))
     return pl.pallas_call(
         step_kernel,
         out_shape=(pltpu.VMEM((8, 8 * SHARD), BF16), pltpu.VMEM((8, 4 * SHARD), BF16), block, block, block),
         in_specs=[pl.BlockSpec(memory_space=pltpu.HBM)] * 4,
         out_specs=(pl.BlockSpec(memory_space=pltpu.VMEM),) * 5,
         scratch_shapes=[
-            block,
+            block, block,
             pltpu.VMEM((16, 8, 128), F32),
             pltpu.VMEM((2, 16, 2, 8, 128), F32),
-            each, each, each, each, dma((3, 2, N_CHUNK)),
-            dma((2, 2)), dma((2, 2, N_CHUNK)), dma((2, 2)), each, dma((4, 2)), dma((4, 2)), dma((6,)),
+            dma((2, 2, N_CHUNK)), dma((2, N_CHUNK)), dma((2,)), dma, dma((4,)), dma((2, 2)), dma((2, 2)), dma((4, 2)), dma((4, 2)), dma((6,)),
             pltpu.SemaphoreType.REGULAR, pltpu.SemaphoreType.REGULAR,
         ],
         compiler_params=pltpu.CompilerParams(collective_id=0, has_side_effects=True, vmem_limit_bytes=STEP_LIMIT),
@@ -404,10 +398,10 @@
         for route in range(2):
             for chunk in range(N_CHUNK):
                 copies += [(src, dst) for dst, src in row_views(array, 0, route, chunk, block.at[route, chunk], chunk < N_TOP)]
-    for index, (src, dst) in enumerate(copies):
-        pltpu.make_async_copy(src, dst, sem.at[index]).start()
-    for index, (src, dst) in enumerate(copies):
-        pltpu.make_async_copy(src, dst, sem.at[index]).wait()
+    for src, dst in copies:
+        pltpu.make_async_copy(src, dst, sem).start()
+    for src, dst in copies:
+        pltpu.make_async_copy(src, dst, sem).wait()
 
 
 def write_out(*blocks):
@@ -417,7 +411,7 @@
         out_shape=(jax.ShapeDtypeStruct((12, 8 * SHARD), BF16), state, state, state),
         in_specs=[pl.BlockSpec(memory_space=pltpu.VMEM)] * 5,
         out_specs=(pl.BlockSpec(memory_space=pltpu.HBM),) * 4,
-        scratch_shapes=[pltpu.SemaphoreType.DMA((24 + 6 * (N_TOP + 2 * N_BOT),))],
+        scratch_shapes=[pltpu.SemaphoreType.DMA],
         compiler_params=pltpu.CompilerParams(vmem_limit_bytes=WRITE_LIMIT),
         name='write_out',
     )(*[pltpu.with_memory_space_constraint(block, pltpu.VMEM) for block in blocks])

time: 381 us -> 379 us (level)
  no operation moved by 1% of the time
where the time goes in v6:
time: 379 us
  Pallas kernels  378 us (100%)
    pallas_call x1, Pallas kernels, run_step(): pl.pallas_call(step_kernel, out_shape=(pltpu.VMEM((8, 8 * SHARD), BF16),...  363 us
    pallas_call x1, Pallas kernels, write_out(): pl.pallas_call(write_kernel, out_shape=(jax.ShapeDtypeStruct((12, 8 * SHA...  15.7 us

profile of v6, /device:TPU:0, one launch (start us, length us, event | category | flops | bytes accessed | tf_op | source)
XLA Modules:
  0.0 378.8 jit_solution(119498619785913979)
XLA Ops:
  0.6 362.5 %lamb_step.1 = (bf16[8,1179648]{1,0:T(8,128)(2,1)S(1)}, bf16[8,589824]{1,0:T(8,128)(2,1)S(1)}, f32[2,9,8,12288]{3,2,1,0:T(8,128)S(1)}, f32[2,9,8,12288]{3,2,1,0:T(8,128)S(1)}, f32[2,9,8,12288]{3,2,1,0:T(8,128)S(1)}) custom-call(bf16[1,12,1179648]{2,1,0:T(8,128)(2,1)} %grads.1, f32[12,147456]{1,0:T(8,128)} %master_in.1, f32[12,147456]{1,0:T(8,128)} %one_in.1, ...), custom_call_target="tpu_custom_call" | custom-call | tf_op jit(solution)/shard_map/lamb_step/pallas_call | solution.py:374
  363.2 15.7 %write_out.1 = (bf16[12,1179648]{1,0:T(8,128)(2,1)}, f32[12,147456]{1,0:T(8,128)}, f32[12,147456]{1,0:T(8,128)}, f32[12,147456]{1,0:T(8,128)}) custom-call(bf16[8,1179648]{1,0:T(8,128)(2,1)S(1)} %get-tuple-element.9.top, bf16[8,589824]{1,0:T(8,128)(2,1)S(1)} %get-tuple-element.10.bot, f32[2,9,8,12288]{3,2,1,0:T(8,128)S(1)} %get-tuple-element.11.master, ...), custom_call_target="tpu_custom_call" | custom-call | tf_op jit(solution)/shard_map/write_out/pallas_call | solution.py:409

commit v7 on v6

--- a/solution.py
+++ b/solution.py
@@ -50,13 +50,6 @@
     return (pos_y * 2 + pos_x) * 2 + core
 
 
-def others():
-    mine = lax.axis_index('model') * 8 + lax.axis_index('data')
-    for step in range(1, 16):
-        other = lax.rem(mine + step, 16)
-        yield other // 8, lax.rem(other, 8)
-
-
 def drain(ref, sem):
     pltpu.make_async_copy(ref, ref, sem).wait()
 
@@ -93,7 +86,7 @@
 def step_kernel(
     grads, master_in, one_in, two_in,
     top_out, bot_out, master, one, two,
-    mean, sent, total_box, norm_box,
+    mean, sent, total_box, bot_box, top_box,
     near_recv, corner_recv, first_send, second_send, load_sem, side_send, forward_send, partner_send, partner_recv, box_sem, seen, known,
 ):
     pos_y, pos_x, core = my_place()
@@ -214,11 +207,16 @@
             load(two_in, two, load_sem.at[2 + int(top)], route, chunk, top)
         return squares
 
+    everyone = [(row, data_index(*chip, side)) for row, chip in (
+        (flip(model_pos), chips[3]), (flip(model_pos), chips[2]), (flip(model_pos), chips[1]), (model_pos, chips[3]),
+        (flip(model_pos), chips[0]), (model_pos, chips[2]), (model_pos, chips[1]),
+    ) for side in (core, flip(core))] + [(model_pos, partner)]
+
     def share_all(box, send_sem, recv_sem):
-        for device in others():
+        for device in everyone:
             pltpu.make_async_remote_copy(src_ref=box.at[mine], dst_ref=box.at[mine], send_sem=send_sem, recv_sem=recv_sem, device_id=device, device_id_type=MESH).start()
 
-    total_box[mine] = sweep(finish, zero)
+    total_box[mine] = jnp.sum(sweep(finish, zero), axis=0, keepdims=True)
     pl.semaphore_wait(known, 1)
     share_all(total_box, box_sem.at[0], box_sem.at[1])
     drain(total_box.at[pl.ds(0, 15)], box_sem.at[1])
@@ -244,35 +242,36 @@
 
         return strips(body, carry, UPDATE_STRIP)
 
-    def update_rows(index, low, high, weight_squares):
+    def update_rows(index, low, high):
         drain(two.at[:, pl.ds(low, high - low)], load_sem.at[2 + index])
-        box = norm_box.at[index]
-        box[mine, 0] = weight_squares
-        box[mine, 1] = lax.fori_loop(low, high, lambda chunk, total: update(1, chunk, update(0, chunk, total)), zero)
+        return lax.fori_loop(low, high, lambda chunk, total: update(1, chunk, update(0, chunk, total)), zero)
+
+    def share_norms(index, box, rows):
+        for position, value in enumerate(rows):
+            box[mine, position:position + 1] = value
         share_all(box, box_sem.at[2 + index], box_sem.at[4 + index])
 
-    def row_sums(index):
-        box = norm_box.at[index]
+    def norm_rows(index, box):
         drain(box.at[pl.ds(0, 15)], box_sem.at[4 + index])
-        return jnp.sum(jnp.sum(box[...], axis=0), axis=2, keepdims=True)
+        return jnp.sqrt(jnp.sum(jnp.sum(box[...], axis=0), axis=1, keepdims=True))
 
     def bot_rate():
-        sums = jnp.sqrt(jnp.sum(row_sums(0), axis=1, keepdims=True))
-        return LEARN_RATE * (sums[0] / sums[1]) + jnp.zeros((8, 1), F32)
+        norms = norm_rows(0, bot_box)
+        return LEARN_RATE * (norms[0:1] / norms[1:2]) + jnp.zeros((8, 1), F32)
 
     def top_rate():
-        sums = row_sums(1)
+        norms = norm_rows(1, top_box)
+        rates = [LEARN_RATE * (norms[position:position + 1] / norms[position + 3:position + 4]) for position in range(3)]
         row = lax.broadcasted_iota(jnp.int32, (8, 1), 0)
-
-        def norms(values):
-            pieces = [jnp.sum(jnp.where(mask, values, 0.0), axis=0, keepdims=True) for mask in (row < 3, row == 3, row > 3)]
-            return jnp.sqrt(jnp.where(row < 3, pieces[0], jnp.where(row == 3, pieces[1], pieces[2])))
-
-        return LEARN_RATE * (norms(sums[0]) / norms(sums[1]))
+        return jnp.where(row < 3, rates[0], jnp.where(row == 3, rates[1], rates[2]))
+
+    def tensor_rows(squares):
+        row = lax.broadcasted_iota(jnp.int32, (8, 128), 0)
+        return [jnp.sum(jnp.where(mask, squares, 0.0), axis=0, keepdims=True) for mask in (row < 3, row == 3, row > 3)]
 
     drain(one, load_sem.at[1])
-    update_rows(0, N_TOP, N_CHUNK, bot_squares)
-    update_rows(1, 0, N_TOP, top_squares)
+    share_norms(0, bot_box, [jnp.sum(squares, axis=0, keepdims=True) for squares in (bot_squares, update_rows(0, N_TOP, N_CHUNK))])
+    share_norms(1, top_box, tensor_rows(top_squares) + tensor_rows(update_rows(1, 0, N_TOP)))
 
     def piece(place, route, chunk, top):
         if top:
@@ -356,8 +355,8 @@
             drain(part(places[chip], top), partner_send.at[chip, kind])
             drain(part(data_index(row_pos, col_pos, flip(core)), top), partner_recv.at[chip, kind])
     drain(total_box.at[pl.ds(0, 15)], box_sem.at[0])
-    for index in range(2):
-        drain(norm_box.at[index, pl.ds(0, 15)], box_sem.at[2 + index])
+    drain(bot_box.at[pl.ds(0, 15)], box_sem.at[2])
+    drain(top_box.at[pl.ds(0, 15)], box_sem.at[3])
 
     drain(top_out.at[:, pl.ds(0, 6 * SHARD)], first_send.at[1])
     drain(bot_out.at[:, pl.ds(0, 3 * SHARD)], first_send.at[0])
@@ -378,8 +377,9 @@
         out_specs=(pl.BlockSpec(memory_space=pltpu.VMEM),) * 5,
         scratch_shapes=[
             block, block,
-            pltpu.VMEM((16, 8, 128), F32),
-            pltpu.VMEM((2, 16, 2, 8, 128), F32),
+            pltpu.VMEM((16, 1, 128), F32),
+            pltpu.VMEM((16, 2, 128), F32),
+            pltpu.VMEM((16, 6, 128), F32),
             dma((2, 2, N_CHUNK)), dma((2, N_CHUNK)), dma((2,)), dma, dma((4,)), dma((2, 2)), dma((2, 2)), dma((4, 2)), dma((4, 2)), dma((6,)),
             pltpu.SemaphoreType.REGULAR, pltpu.SemaphoreType.REGULAR,
         ],

time: 379 us -> 379 us (level)
  no operation moved by 1% of the time
where the time goes in v7:
time: 379 us
  Pallas kernels  378 us (100%)
    pallas_call x1, Pallas kernels, run_step(): pl.pallas_call(step_kernel, out_shape=(pltpu.VMEM((8, 8 * SHARD), BF16),...  362 us
    pallas_call x1, Pallas kernels, write_out(): pl.pallas_call(write_kernel, out_shape=(jax.ShapeDtypeStruct((12, 8 * SHA...  15.7 us

profile of v7, /device:TPU:0, one launch (start us, length us, event | category | flops | bytes accessed | tf_op | source)
XLA Modules:
  0.0 378.7 jit_solution(757317282359806842)
XLA Ops:
  0.6 362.3 %lamb_step.1 = (bf16[8,1179648]{1,0:T(8,128)(2,1)S(1)}, bf16[8,589824]{1,0:T(8,128)(2,1)S(1)}, f32[2,9,8,12288]{3,2,1,0:T(8,128)S(1)}, f32[2,9,8,12288]{3,2,1,0:T(8,128)S(1)}, f32[2,9,8,12288]{3,2,1,0:T(8,128)S(1)}) custom-call(bf16[1,12,1179648]{2,1,0:T(8,128)(2,1)} %grads.1, f32[12,147456]{1,0:T(8,128)} %master_in.1, f32[12,147456]{1,0:T(8,128)} %one_in.1, ...), custom_call_target="tpu_custom_call" | custom-call | tf_op jit(solution)/shard_map/lamb_step/pallas_call | solution.py:373
  363.0 15.7 %write_out.1 = (bf16[12,1179648]{1,0:T(8,128)(2,1)}, f32[12,147456]{1,0:T(8,128)}, f32[12,147456]{1,0:T(8,128)}, f32[12,147456]{1,0:T(8,128)}) custom-call(bf16[8,1179648]{1,0:T(8,128)(2,1)S(1)} %get-tuple-element.9.top, bf16[8,589824]{1,0:T(8,128)(2,1)S(1)} %get-tuple-element.10.bot, f32[2,9,8,12288]{3,2,1,0:T(8,128)S(1)} %get-tuple-element.11.master, ...), custom_call_target="tpu_custom_call" | custom-call | tf_op jit(solution)/shard_map/write_out/pallas_call | solution.py:409

commit v8 on v7

--- a/solution.py
+++ b/solution.py
@@ -86,8 +86,8 @@
 def step_kernel(
     grads, master_in, one_in, two_in,
     top_out, bot_out, master, one, two,
-    mean, sent, total_box, bot_box, top_box,
-    near_recv, corner_recv, first_send, second_send, load_sem, side_send, forward_send, partner_send, partner_recv, box_sem, seen, known,
+    mean, sent, lead, total_box, bot_box, top_box,
+    lead_sem, near_recv, corner_recv, first_send, second_send, load_sem, side_send, forward_send, partner_send, partner_recv, box_sem, seen, known,
 ):
     pos_y, pos_x, core = my_place()
     model_pos = lax.axis_index('model')
@@ -128,7 +128,12 @@
                     to_core = lax.rem(core + other, 2)
                     shard = data_index(*wanted(route, row, col, far), to_core)
                     for src, dst in row_views(grad, shard, route, chunk, landing(route, chunk, 4 + 2 * other + far, 1, top), top):
-                        copy_to(src, dst, data_index(row, col, to_core), first_send.at[int(top)], first_recv.at[route, chunk])
+                        if top and far == other == 0:
+                            @pl.when(chunk > 0)
+                            def _():
+                                copy_to(src, dst, data_index(row, col, to_core), first_send.at[1], first_recv.at[route, chunk])
+                        else:
+                            copy_to(src, dst, data_index(row, col, to_core), first_send.at[int(top)], first_recv.at[route, chunk])
             for route in range(2):
                 shard = data_index(*wanted(route, pos_y, pos_x, far), flip(core))
                 for src, dst in row_views(grad, shard, route, chunk, landing(route, chunk, 2 + far, 1, top), top):
@@ -147,9 +152,18 @@
 
     barrier = pltpu.get_barrier_semaphore()
     tell(barrier, next_to)
+    leads = []
+    for route in range(2):
+        shard = data_index(*wanted(route, *chips[1 + route], 0), core)
+        (src, _), = row_views(grad, shard, route, 0, lead.at[route], True)
+        leads.append(pltpu.make_async_copy(src, lead.at[route], lead_sem.at[route]))
+        leads[-1].start()
+    pl.semaphore_wait(barrier, len(next_to))
+    for route, copy in enumerate(leads):
+        copy.wait()
+        copy_to(lead.at[route], landing(route, 0, 4, 1, True), places[1 + route], first_send.at[1], first_recv.at[route, 0])
+    sweep(remote)
     sweep(local)
-    pl.semaphore_wait(barrier, len(next_to))
-    sweep(remote)
     tell(seen, next_to)
 
     def load_state(chunk, carry, top):
@@ -376,11 +390,11 @@
         in_specs=[pl.BlockSpec(memory_space=pltpu.HBM)] * 4,
         out_specs=(pl.BlockSpec(memory_space=pltpu.VMEM),) * 5,
         scratch_shapes=[
-            block, block,
+            block, block, pltpu.VMEM((2, 8, COLS), BF16),
             pltpu.VMEM((16, 1, 128), F32),
             pltpu.VMEM((16, 2, 128), F32),
             pltpu.VMEM((16, 6, 128), F32),
-            dma((2, 2, N_CHUNK)), dma((2, N_CHUNK)), dma((2,)), dma, dma((4,)), dma((2, 2)), dma((2, 2)), dma((4, 2)), dma((4, 2)), dma((6,)),
+            dma((2,)), dma((2, 2, N_CHUNK)), dma((2, N_CHUNK)), dma((2,)), dma, dma((4,)), dma((2, 2)), dma((2, 2)), dma((4, 2)), dma((4, 2)), dma((6,)),
             pltpu.SemaphoreType.REGULAR, pltpu.SemaphoreType.REGULAR,
         ],
         compiler_params=pltpu.CompilerParams(collective_id=0, has_side_effects=True, vmem_limit_bytes=STEP_LIMIT),

time: 379 us -> 379 us (level)
  no operation moved by 1% of the time
where the time goes in v8:
time: 379 us
  Pallas kernels  378 us (100%)
    pallas_call x1, Pallas kernels, run_step(): pl.pallas_call(step_kernel, out_shape=(pltpu.VMEM((8, 8 * SHARD), BF16),...  362 us
    pallas_call x1, Pallas kernels, write_out(): pl.pallas_call(write_kernel, out_shape=(jax.ShapeDtypeStruct((12, 8 * SHA...  15.7 us

profile of v8, /device:TPU:0, one launch (start us, length us, event | category | flops | bytes accessed | tf_op | source)
XLA Modules:
  0.0 378.8 jit_solution(15044524015263019506)
XLA Ops:
  0.6 362.5 %lamb_step.1 = (bf16[8,1179648]{1,0:T(8,128)(2,1)S(1)}, bf16[8,589824]{1,0:T(8,128)(2,1)S(1)}, f32[2,9,8,12288]{3,2,1,0:T(8,128)S(1)}, f32[2,9,8,12288]{3,2,1,0:T(8,128)S(1)}, f32[2,9,8,12288]{3,2,1,0:T(8,128)S(1)}) custom-call(bf16[1,12,1179648]{2,1,0:T(8,128)(2,1)} %grads.1, f32[12,147456]{1,0:T(8,128)} %master_in.1, f32[12,147456]{1,0:T(8,128)} %one_in.1, ...), custom_call_target="tpu_custom_call" | custom-call | tf_op jit(solution)/shard_map/lamb_step/pallas_call | solution.py:387
  363.1 15.7 %write_out.1 = (bf16[12,1179648]{1,0:T(8,128)(2,1)}, f32[12,147456]{1,0:T(8,128)}, f32[12,147456]{1,0:T(8,128)}, f32[12,147456]{1,0:T(8,128)}) custom-call(bf16[8,1179648]{1,0:T(8,128)(2,1)S(1)} %get-tuple-element.9.top, bf16[8,589824]{1,0:T(8,128)(2,1)S(1)} %get-tuple-element.10.bot, f32[2,9,8,12288]{3,2,1,0:T(8,128)S(1)} %get-tuple-element.11.master, ...), custom_call_target="tpu_custom_call" | custom-call | tf_op jit(solution)/shard_map/write_out/pallas_call | solution.py:423

commit v9 on v7

--- a/solution.py
+++ b/solution.py
@@ -22,7 +22,7 @@
 BF16 = jnp.bfloat16
 
 SHARD = 147456
-COLS = 12288
+COLS = 18432
 TOP_ROUTE = SHARD // 2
 BOT_ROUTE = SHARD // 4
 N_TOP = TOP_ROUTE // COLS

time: 379 us -> 380 us (level)
  no operation moved by 1% of the time
where the time goes in v9:
time: 380 us
  Pallas kernels  379 us (100%)
    pallas_call x1, Pallas kernels, run_step(): pl.pallas_call(step_kernel, out_shape=(pltpu.VMEM((8, 8 * SHARD), BF16),...  363 us
    pallas_call x1, Pallas kernels, write_out(): pl.pallas_call(write_kernel, out_shape=(jax.ShapeDtypeStruct((12, 8 * SHA...  15.7 us

profile of v9, /device:TPU:0, one launch (start us, length us, event | category | flops | bytes accessed | tf_op | source)
XLA Modules:
  0.0 379.8 jit_solution(16303012202769765538)
XLA Ops:
  0.6 363.5 %lamb_step.1 = (bf16[8,1179648]{1,0:T(8,128)(2,1)S(1)}, bf16[8,589824]{1,0:T(8,128)(2,1)S(1)}, f32[2,6,8,18432]{3,2,1,0:T(8,128)S(1)}, f32[2,6,8,18432]{3,2,1,0:T(8,128)S(1)}, f32[2,6,8,18432]{3,2,1,0:T(8,128)S(1)}) custom-call(bf16[1,12,1179648]{2,1,0:T(8,128)(2,1)} %grads.1, f32[12,147456]{1,0:T(8,128)} %master_in.1, f32[12,147456]{1,0:T(8,128)} %one_in.1, ...), custom_call_target="tpu_custom_call" | custom-call | tf_op jit(solution)/shard_map/lamb_step/pallas_call | solution.py:373
  364.1 15.7 %write_out.1 = (bf16[12,1179648]{1,0:T(8,128)(2,1)}, f32[12,147456]{1,0:T(8,128)}, f32[12,147456]{1,0:T(8,128)}, f32[12,147456]{1,0:T(8,128)}) custom-call(bf16[8,1179648]{1,0:T(8,128)(2,1)S(1)} %get-tuple-element.9.top, bf16[8,589824]{1,0:T(8,128)(2,1)S(1)} %get-tuple-element.10.bot, f32[2,6,8,18432]{3,2,1,0:T(8,128)S(1)} %get-tuple-element.11.master, ...), custom_call_target="tpu_custom_call" | custom-call | tf_op jit(solution)/shard_map/write_out/pallas_call | solution.py:409

commit v10 on v9

--- a/solution.py
+++ b/solution.py
@@ -22,7 +22,7 @@
 BF16 = jnp.bfloat16
 
 SHARD = 147456
-COLS = 18432
+COLS = 6144
 TOP_ROUTE = SHARD // 2
 BOT_ROUTE = SHARD // 4
 N_TOP = TOP_ROUTE // COLS

time: 380 us -> 378 us (level)
  no operation moved by 1% of the time
where the time goes in v10:
time: 378 us
  Pallas kernels  377 us (100%)
    pallas_call x1, Pallas kernels, run_step(): pl.pallas_call(step_kernel, out_shape=(pltpu.VMEM((8, 8 * SHARD), BF16),...  362 us
    pallas_call x1, Pallas kernels, write_out(): pl.pallas_call(write_kernel, out_shape=(jax.ShapeDtypeStruct((12, 8 * SHA...  15.7 us

profile of v10, /device:TPU:0, one launch (start us, length us, event | category | flops | bytes accessed | tf_op | source)
XLA Modules:
  0.0 378.0 jit_solution(7813192361741900774)
XLA Ops:
  0.6 361.7 %lamb_step.1 = (bf16[8,1179648]{1,0:T(8,128)(2,1)S(1)}, bf16[8,589824]{1,0:T(8,128)(2,1)S(1)}, f32[2,18,8,6144]{3,2,1,0:T(8,128)S(1)}, f32[2,18,8,6144]{3,2,1,0:T(8,128)S(1)}, f32[2,18,8,6144]{3,2,1,0:T(8,128)S(1)}) custom-call(bf16[1,12,1179648]{2,1,0:T(8,128)(2,1)} %grads.1, f32[12,147456]{1,0:T(8,128)} %master_in.1, f32[12,147456]{1,0:T(8,128)} %one_in.1, ...), custom_call_target="tpu_custom_call" | custom-call | tf_op jit(solution)/shard_map/lamb_step/pallas_call | solution.py:373
  362.4 15.7 %write_out.1 = (bf16[12,1179648]{1,0:T(8,128)(2,1)}, f32[12,147456]{1,0:T(8,128)}, f32[12,147456]{1,0:T(8,128)}, f32[12,147456]{1,0:T(8,128)}) custom-call(bf16[8,1179648]{1,0:T(8,128)(2,1)S(1)} %get-tuple-element.9.top, bf16[8,589824]{1,0:T(8,128)(2,1)S(1)} %get-tuple-element.10.bot, f32[2,18,8,6144]{3,2,1,0:T(8,128)S(1)} %get-tuple-element.11.master, ...), custom_call_target="tpu_custom_call" | custom-call | tf_op jit(solution)/shard_map/write_out/pallas_call | solution.py:409

commit v11 on v10

--- a/solution.py
+++ b/solution.py
@@ -28,6 +28,7 @@
 N_TOP = TOP_ROUTE // COLS
 N_BOT = BOT_ROUTE // COLS
 N_CHUNK = N_TOP + N_BOT
+HOLD = N_CHUNK - 2
 STRIP = 1024
 UPDATE_STRIP = 2048
 
@@ -178,21 +179,24 @@
         return strips(body, squares)
 
     def first_sums(chunk, squares, top):
-        squares = add_four(0, chunk, squares, top)
-
-        @pl.when(chunk > 0)
+        squares = add_four(1, chunk, add_four(0, chunk, squares, top), top)
+
+        @pl.when(chunk >= HOLD)
         def _():
-            second(1, chunk - 1)
-
-        squares = add_four(1, chunk, squares, top)
-        second(0, chunk)
+            second(0, chunk - HOLD)
+            second(1, chunk - HOLD)
+
         return squares
 
     drain(master, load_sem.at[0])
     zero = jnp.zeros((8, 128), F32)
     top_squares = lax.fori_loop(0, N_TOP, functools.partial(first_sums, top=True), zero)
     bot_squares = lax.fori_loop(N_TOP, N_CHUNK, functools.partial(first_sums, top=False), zero)
-    second(1, N_CHUNK - 1)
+
+    @pl.loop(N_CHUNK - HOLD, N_CHUNK)
+    def _(chunk):
+        second(0, chunk)
+        second(1, chunk)
 
     def finish(chunk, squares, top):
         for route in range(2):
@@ -325,8 +329,6 @@
             for axis in range(2):
                 view = piece(places[1 + axis], route, chunk, top)
                 drain(view, near_recv.at[axis, route, chunk])
-                if axis == route:
-                    copy_to(view, view, places[2 - axis], forward_send.at[route, kind], corner_recv.at[route, chunk])
                 copy_to(view, view, partner, partner_send.at[1 + axis, kind], partner_recv.at[1 + axis, kind])
         return carry
 
@@ -343,7 +345,17 @@
 
     lax.fori_loop(N_TOP, N_CHUNK, functools.partial(own, top=False), bot_rate())
     lax.fori_loop(0, N_TOP, functools.partial(own, top=True), top_rate())
-    bottom_first(hand_on)
+    def hand_to_corner(chunk, carry, top):
+        for route in range(2):
+            view = piece(places[1 + route], route, chunk, top)
+            copy_to(view, view, places[2 - route], forward_send.at[route, int(top)], corner_recv.at[route, chunk])
+        return carry
+
+    lax.fori_loop(N_TOP, N_CHUNK, functools.partial(hand_on, top=False), 0)
+    lax.fori_loop(0, N_TOP - 2, functools.partial(hand_on, top=True), 0)
+    lax.fori_loop(N_TOP, N_CHUNK, functools.partial(hand_to_corner, top=False), 0)
+    lax.fori_loop(0, N_TOP - 2, functools.partial(hand_to_corner, top=True), 0)
+    lax.fori_loop(N_TOP - 2, N_TOP, lambda chunk, carry: hand_to_corner(chunk, hand_on(chunk, carry, True), True), 0)
     bottom_first(corner)
 
     for top in (True, False):

time: 378 us -> 378 us (level)
  no operation moved by 1% of the time
where the time goes in v11:
time: 378 us
  Pallas kernels  377 us (100%)
    pallas_call x1, Pallas kernels, run_step(): pl.pallas_call(step_kernel, out_shape=(pltpu.VMEM((8, 8 * SHARD), BF16),...  362 us
    pallas_call x1, Pallas kernels, write_out(): pl.pallas_call(write_kernel, out_shape=(jax.ShapeDtypeStruct((12, 8 * SHA...  15.7 us

profile of v11, /device:TPU:0, one launch (start us, length us, event | category | flops | bytes accessed | tf_op | source)
XLA Modules:
  0.0 378.0 jit_solution(2090622282389186123)
XLA Ops:
  0.6 361.7 %lamb_step.1 = (bf16[8,1179648]{1,0:T(8,128)(2,1)S(1)}, bf16[8,589824]{1,0:T(8,128)(2,1)S(1)}, f32[2,18,8,6144]{3,2,1,0:T(8,128)S(1)}, f32[2,18,8,6144]{3,2,1,0:T(8,128)S(1)}, f32[2,18,8,6144]{3,2,1,0:T(8,128)S(1)}) custom-call(bf16[1,12,1179648]{2,1,0:T(8,128)(2,1)} %grads.1, f32[12,147456]{1,0:T(8,128)} %master_in.1, f32[12,147456]{1,0:T(8,128)} %one_in.1, ...), custom_call_target="tpu_custom_call" | custom-call | tf_op jit(solution)/shard_map/lamb_step/pallas_call | solution.py:385
  362.4 15.7 %write_out.1 = (bf16[12,1179648]{1,0:T(8,128)(2,1)}, f32[12,147456]{1,0:T(8,128)}, f32[12,147456]{1,0:T(8,128)}, f32[12,147456]{1,0:T(8,128)}) custom-call(bf16[8,1179648]{1,0:T(8,128)(2,1)S(1)} %get-tuple-element.9.top, bf16[8,589824]{1,0:T(8,128)(2,1)S(1)} %get-tuple-element.10.bot, f32[2,18,8,6144]{3,2,1,0:T(8,128)S(1)} %get-tuple-element.11.master, ...), custom_call_target="tpu_custom_call" | custom-call | tf_op jit(solution)/shard_map/write_out/pallas_call | solution.py:421

commit v12 on v10

--- a/solution.py
+++ b/solution.py
@@ -28,6 +28,14 @@
 N_TOP = TOP_ROUTE // COLS
 N_BOT = BOT_ROUTE // COLS
 N_CHUNK = N_TOP + N_BOT
+REDUCE_GROUPS = (
+    (0, N_TOP // 2, True), (N_TOP // 2, N_TOP, True),
+    (N_TOP, N_TOP + N_BOT // 2, False), (N_TOP + N_BOT // 2, N_CHUNK - 1, False), (N_CHUNK - 1, N_CHUNK, False),
+)
+GATHER_GROUPS = (
+    (N_TOP, N_TOP + N_BOT // 2, False), (N_TOP + N_BOT // 2, N_CHUNK, False),
+    (0, N_TOP // 2, True), (N_TOP // 2, N_TOP - 2, True), (N_TOP - 2, N_TOP - 1, True), (N_TOP - 1, N_TOP, True),
+)
 STRIP = 1024
 UPDATE_STRIP = 2048
 
@@ -66,8 +74,9 @@
 
 
 def sweep(body, carry=0):
-    carry = lax.fori_loop(0, N_TOP, functools.partial(body, top=True), carry)
-    return lax.fori_loop(N_TOP, N_CHUNK, functools.partial(body, top=False), carry)
+    for index, (low, high, top) in enumerate(REDUCE_GROUPS):
+        carry = lax.fori_loop(low, high, functools.partial(body, index=index, top=top), carry)
+    return carry
 
 
 def strips(body, carry=0, width=STRIP):
@@ -112,15 +121,15 @@
     def wanted(route, row, col, far):
         return (lax.rem(row + far, 2), col) if route == 0 else (row, lax.rem(col + far, 2))
 
-    def local(chunk, carry, top):
+    def local(chunk, carry, index, top):
         for route in range(2):
             for far in range(2):
                 shard = data_index(*wanted(route, pos_y, pos_x, far), core)
                 for src, dst in row_views(grad, shard, route, chunk, landing(route, chunk, far, 1, top), top):
-                    pltpu.make_async_copy(src, dst, first_recv.at[route, chunk]).start()
+                    pltpu.make_async_copy(src, dst, first_recv.at[route, index]).start()
         return carry
 
-    def remote(chunk, carry, top):
+    def remote(chunk, carry, index, top):
         for far in range(2):
             for other in range(2):
                 for route in range(2):
@@ -128,11 +137,11 @@
                     to_core = lax.rem(core + other, 2)
                     shard = data_index(*wanted(route, row, col, far), to_core)
                     for src, dst in row_views(grad, shard, route, chunk, landing(route, chunk, 4 + 2 * other + far, 1, top), top):
-                        copy_to(src, dst, data_index(row, col, to_core), first_send.at[int(top)], first_recv.at[route, chunk])
+                        copy_to(src, dst, data_index(row, col, to_core), first_send.at[int(top)], first_recv.at[route, index])
             for route in range(2):
                 shard = data_index(*wanted(route, pos_y, pos_x, far), flip(core))
                 for src, dst in row_views(grad, shard, route, chunk, landing(route, chunk, 2 + far, 1, top), top):
-                    copy_to(src, dst, partner, first_send.at[int(top)], first_recv.at[route, chunk])
+                    copy_to(src, dst, partner, first_send.at[int(top)], first_recv.at[route, index])
         return carry
 
     def load(array, block, sem, route, chunk, top):
@@ -152,7 +161,7 @@
     sweep(remote)
     tell(seen, next_to)
 
-    def load_state(chunk, carry, top):
+    def load_state(chunk, carry, index, top):
         for route in range(2):
             load(master_in, master, load_sem.at[0], route, chunk, top)
             load(one_in, one, load_sem.at[1], route, chunk, top)
@@ -162,42 +171,37 @@
     pl.semaphore_wait(seen, len(next_to))
     tell(known, next_to[-1:])
 
-    def second(route, chunk):
-        copy_to(sent.at[route, chunk], got.at[route, chunk], places[2 - route], second_send, second_recv.at[route, chunk])
-
-    def add_four(route, chunk, squares, top):
-        drain(landing(route, chunk, 0, 8, top), first_recv.at[route, chunk])
-
-        def body(cols, total):
-            for far, target in ((0, mean), (1, sent)):
-                parts = [landing(route, chunk, 2 * source + far, 1, top)[:, cols].astype(F32) for source in range(4)]
-                target[route, chunk, :, cols] = (parts[0] + parts[1]) + (parts[2] + parts[3])
-            weight = master[route, chunk, :, cols]
-            return fold(total, weight * weight)
-
-        return strips(body, squares)
-
-    def first_sums(chunk, squares, top):
-        squares = add_four(0, chunk, squares, top)
-
-        @pl.when(chunk > 0)
-        def _():
-            second(1, chunk - 1)
-
-        squares = add_four(1, chunk, squares, top)
-        second(0, chunk)
+    def second(route, chunk, index):
+        copy_to(sent.at[route, chunk], got.at[route, chunk], places[2 - route], second_send, second_recv.at[route, index])
+
+    def add_four(chunk, squares, top):
+        for route in range(2):
+            def body(cols, total):
+                for far, target in ((0, mean), (1, sent)):
+                    parts = [landing(route, chunk, 2 * source + far, 1, top)[:, cols].astype(F32) for source in range(4)]
+                    target[route, chunk, :, cols] = (parts[0] + parts[1]) + (parts[2] + parts[3])
+                weight = master[route, chunk, :, cols]
+                return fold(total, weight * weight)
+
+            squares = strips(body, squares)
         return squares
 
     drain(master, load_sem.at[0])
     zero = jnp.zeros((8, 128), F32)
-    top_squares = lax.fori_loop(0, N_TOP, functools.partial(first_sums, top=True), zero)
-    bot_squares = lax.fori_loop(N_TOP, N_CHUNK, functools.partial(first_sums, top=False), zero)
-    second(1, N_CHUNK - 1)
+    top_squares = bot_squares = zero
+    for index, (low, high, top) in enumerate(REDUCE_GROUPS):
+        for route in range(2):
+            drain(landing(route, low, 0, 8 * (high - low), top), first_recv.at[route, index])
+        squares = lax.fori_loop(low, high, functools.partial(add_four, top=top), top_squares if top else bot_squares)
+        top_squares, bot_squares = (squares, bot_squares) if top else (top_squares, squares)
+
+        @pl.loop(low, high)
+        def _(chunk):
+            second(0, chunk, index)
+            second(1, chunk, index)
 
     def finish(chunk, squares, top):
         for route in range(2):
-            drain(got.at[route, chunk], second_recv.at[route, chunk])
-
             def body(cols, total):
                 value = (mean[route, chunk, :, cols] + got[route, chunk, :, cols]) * 0.125
                 mean[route, chunk, :, cols] = value
@@ -207,6 +211,14 @@
             load(two_in, two, load_sem.at[2 + int(top)], route, chunk, top)
         return squares
 
+    def finish_all():
+        squares = zero
+        for index, (low, high, top) in enumerate(REDUCE_GROUPS):
+            for route in range(2):
+                drain(got.at[route, pl.ds(low, high - low)], second_recv.at[route, index])
+            squares = lax.fori_loop(low, high, functools.partial(finish, top=top), squares)
+        return squares
+
     everyone = [(row, data_index(*chip, side)) for row, chip in (
         (flip(model_pos), chips[3]), (flip(model_pos), chips[2]), (flip(model_pos), chips[1]), (model_pos, chips[3]),
         (flip(model_pos), chips[0]), (model_pos, chips[2]), (model_pos, chips[1]),
@@ -216,7 +228,7 @@
         for device in everyone:
             pltpu.make_async_remote_copy(src_ref=box.at[mine], dst_ref=box.at[mine], send_sem=send_sem, recv_sem=recv_sem, device_id=device, device_id_type=MESH).start()
 
-    total_box[mine] = jnp.sum(sweep(finish, zero), axis=0, keepdims=True)
+    total_box[mine] = jnp.sum(finish_all(), axis=0, keepdims=True)
     pl.semaphore_wait(known, 1)
     share_all(total_box, box_sem.at[0], box_sem.at[1])
     drain(total_box.at[pl.ds(0, 15)], box_sem.at[1])
@@ -273,12 +285,12 @@
     share_norms(0, bot_box, [jnp.sum(squares, axis=0, keepdims=True) for squares in (bot_squares, update_rows(0, N_TOP, N_CHUNK))])
     share_norms(1, top_box, tensor_rows(top_squares) + tensor_rows(update_rows(1, 0, N_TOP)))
 
-    def piece(place, route, chunk, top):
+    def piece(place, route, chunk, top, count=1):
         if top:
             start = place * SHARD + route * TOP_ROUTE + chunk * COLS
         else:
             start = place * (SHARD // 2) + route * BOT_ROUTE + (chunk - N_TOP) * COLS
-        return (top_out if top else bot_out).at[:, pl.ds(pl.multiple_of(start, COLS), COLS)]
+        return (top_out if top else bot_out).at[:, pl.ds(pl.multiple_of(start, COLS), count * COLS)]
 
     def part(place, top, share=1):
         size = SHARD if top else SHARD // 2
@@ -296,55 +308,51 @@
 
         strips(body)
 
-    def send(route, chunk, top):
+    def send(route, chunk, index, top):
         view = piece(places[0], route, chunk, top)
         kind = int(top)
         for axis in range(2):
-            copy_to(view, view, places[1 + axis], side_send.at[axis, kind], near_recv.at[axis, route, chunk])
+            copy_to(view, view, places[1 + axis], side_send.at[axis, kind], near_recv.at[axis, route, index])
         copy_to(view, view, partner, partner_send.at[0, kind], partner_recv.at[0, kind])
 
-    def own(chunk, rate, top):
+    def own(chunk, rate, index, low, high, top):
         weights(0, chunk, rate, top)
 
-        @pl.when(chunk > (0 if top else N_TOP))
+        @pl.when(chunk > low)
         def _():
-            send(1, chunk - 1, top)
+            send(1, chunk - 1, index, top)
 
         weights(1, chunk, rate, top)
-        send(0, chunk, top)
-
-        @pl.when(chunk == (N_TOP - 1 if top else N_CHUNK - 1))
+        send(0, chunk, index, top)
+
+        @pl.when(chunk == high - 1)
         def _():
-            send(1, chunk, top)
+            send(1, chunk, index, top)
 
         return rate
 
-    def hand_on(chunk, carry, top):
+    for index, (low, high, top) in enumerate(GATHER_GROUPS):
+        if index == 0:
+            rate = bot_rate()
+        elif top and not GATHER_GROUPS[index - 1][2]:
+            rate = top_rate()
+        lax.fori_loop(low, high, functools.partial(own, index=index, low=low, high=high, top=top), rate)
+
+    for index, (low, high, top) in enumerate(GATHER_GROUPS):
         kind = int(top)
-        for route in range(2):
-            for axis in range(2):
-                view = piece(places[1 + axis], route, chunk, top)
-                drain(view, near_recv.at[axis, route, chunk])
+        for axis in range(2):
+            for route in range(2):
+                view = piece(places[1 + axis], route, low, top, high - low)
+                drain(view, near_recv.at[axis, route, index])
                 if axis == route:
-                    copy_to(view, view, places[2 - axis], forward_send.at[route, kind], corner_recv.at[route, chunk])
+                    copy_to(view, view, places[2 - route], forward_send.at[route, kind], corner_recv.at[route, index])
                 copy_to(view, view, partner, partner_send.at[1 + axis, kind], partner_recv.at[1 + axis, kind])
-        return carry
-
-    def corner(chunk, carry, top):
-        for route in range(2):
-            view = piece(places[3], route, chunk, top)
-            drain(view, corner_recv.at[route, chunk])
+
+    for index, (low, high, top) in enumerate(GATHER_GROUPS):
+        for route in range(2):
+            view = piece(places[3], route, low, top, high - low)
+            drain(view, corner_recv.at[route, index])
             copy_to(view, view, partner, partner_send.at[3, int(top)], partner_recv.at[3, int(top)])
-        return carry
-
-    def bottom_first(body, carry=0):
-        carry = lax.fori_loop(N_TOP, N_CHUNK, functools.partial(body, top=False), carry)
-        return lax.fori_loop(0, N_TOP, functools.partial(body, top=True), carry)
-
-    lax.fori_loop(N_TOP, N_CHUNK, functools.partial(own, top=False), bot_rate())
-    lax.fori_loop(0, N_TOP, functools.partial(own, top=True), top_rate())
-    bottom_first(hand_on)
-    bottom_first(corner)
 
     for top in (True, False):
         kind = int(top)
@@ -380,7 +388,7 @@
             pltpu.VMEM((16, 1, 128), F32),
             pltpu.VMEM((16, 2, 128), F32),
             pltpu.VMEM((16, 6, 128), F32),
-            dma((2, 2, N_CHUNK)), dma((2, N_CHUNK)), dma((2,)), dma, dma((4,)), dma((2, 2)), dma((2, 2)), dma((4, 2)), dma((4, 2)), dma((6,)),
+            dma((2, 2, len(GATHER_GROUPS))), dma((2, len(GATHER_GROUPS))), dma((2,)), dma, dma((4,)), dma((2, 2)), dma((2, 2)), dma((4, 2)), dma((4, 2)), dma((6,)),
             pltpu.SemaphoreType.REGULAR, pltpu.SemaphoreType.REGULAR,
         ],
         compiler_params=pltpu.CompilerParams(collective_id=0, has_side_effects=True, vmem_limit_bytes=STEP_LIMIT),

time: 378 us -> 377 us (level)
  no operation moved by 1% of the time
where the time goes in v12:
time: 377 us
  Pallas kernels  377 us (100%)
    pallas_call x1, Pallas kernels, run_step(): pl.pallas_call(step_kernel, out_shape=(pltpu.VMEM((8, 8 * SHARD), BF16),...  361 us
    pallas_call x1, Pallas kernels, write_out(): pl.pallas_call(write_kernel, out_shape=(jax.ShapeDtypeStruct((12, 8 * SHA...  15.7 us

profile of v12, /device:TPU:0, one launch (start us, length us, event | category | flops | bytes accessed | tf_op | source)
XLA Modules:
  0.0 377.4 jit_solution(1899737339694699201)
XLA Ops:
  0.6 361.1 %lamb_step.1 = (bf16[8,1179648]{1,0:T(8,128)(2,1)S(1)}, bf16[8,589824]{1,0:T(8,128)(2,1)S(1)}, f32[2,18,8,6144]{3,2,1,0:T(8,128)S(1)}, f32[2,18,8,6144]{3,2,1,0:T(8,128)S(1)}, f32[2,18,8,6144]{3,2,1,0:T(8,128)S(1)}) custom-call(bf16[1,12,1179648]{2,1,0:T(8,128)(2,1)} %grads.1, f32[12,147456]{1,0:T(8,128)} %master_in.1, f32[12,147456]{1,0:T(8,128)} %one_in.1, ...), custom_call_target="tpu_custom_call" | custom-call | tf_op jit(solution)/shard_map/lamb_step/pallas_call | solution.py:381
  361.7 15.7 %write_out.1 = (bf16[12,1179648]{1,0:T(8,128)(2,1)}, f32[12,147456]{1,0:T(8,128)}, f32[12,147456]{1,0:T(8,128)}, f32[12,147456]{1,0:T(8,128)}) custom-call(bf16[8,1179648]{1,0:T(8,128)(2,1)S(1)} %get-tuple-element.9.top, bf16[8,589824]{1,0:T(8,128)(2,1)S(1)} %get-tuple-element.10.bot, f32[2,18,8,6144]{3,2,1,0:T(8,128)S(1)} %get-tuple-element.11.master, ...), custom_call_target="tpu_custom_call" | custom-call | tf_op jit(solution)/shard_map/write_out/pallas_call | solution.py:417

commit v13 on v12

--- a/solution.py
+++ b/solution.py
@@ -22,7 +22,7 @@
 BF16 = jnp.bfloat16
 
 SHARD = 147456
-COLS = 6144
+COLS = 3072
 TOP_ROUTE = SHARD // 2
 BOT_ROUTE = SHARD // 4
 N_TOP = TOP_ROUTE // COLS
@@ -37,7 +37,7 @@
     (0, N_TOP // 2, True), (N_TOP // 2, N_TOP - 2, True), (N_TOP - 2, N_TOP - 1, True), (N_TOP - 1, N_TOP, True),
 )
 STRIP = 1024
-UPDATE_STRIP = 2048
+UPDATE_STRIP = 3072
 
 TINY = 1.2e-38
 MIB = 1024 * 1024

time: 377 us -> 377 us (level)
  no operation moved by 1% of the time
where the time goes in v13:
time: 377 us
  Pallas kernels  376 us (100%)
    pallas_call x1, Pallas kernels, run_step(): pl.pallas_call(step_kernel, out_shape=(pltpu.VMEM((8, 8 * SHARD), BF16),...  360 us
    pallas_call x1, Pallas kernels, write_out(): pl.pallas_call(write_kernel, out_shape=(jax.ShapeDtypeStruct((12, 8 * SHA...  15.7 us

profile of v13, /device:TPU:0, one launch (start us, length us, event | category | flops | bytes accessed | tf_op | source)
XLA Modules:
  0.0 376.6 jit_solution(1169593948024348256)
XLA Ops:
  0.6 360.3 %lamb_step.1 = (bf16[8,1179648]{1,0:T(8,128)(2,1)S(1)}, bf16[8,589824]{1,0:T(8,128)(2,1)S(1)}, f32[2,36,8,3072]{3,2,1,0:T(8,128)S(1)}, f32[2,36,8,3072]{3,2,1,0:T(8,128)S(1)}, f32[2,36,8,3072]{3,2,1,0:T(8,128)S(1)}) custom-call(bf16[1,12,1179648]{2,1,0:T(8,128)(2,1)} %grads.1, f32[12,147456]{1,0:T(8,128)} %master_in.1, f32[12,147456]{1,0:T(8,128)} %one_in.1, ...), custom_call_target="tpu_custom_call" | custom-call | tf_op jit(solution)/shard_map/lamb_step/pallas_call | solution.py:381
  360.9 15.7 %write_out.1 = (bf16[12,1179648]{1,0:T(8,128)(2,1)}, f32[12,147456]{1,0:T(8,128)}, f32[12,147456]{1,0:T(8,128)}, f32[12,147456]{1,0:T(8,128)}) custom-call(bf16[8,1179648]{1,0:T(8,128)(2,1)S(1)} %get-tuple-element.9.top, bf16[8,589824]{1,0:T(8,128)(2,1)S(1)} %get-tuple-element.10.bot, f32[2,36,8,3072]{3,2,1,0:T(8,128)S(1)} %get-tuple-element.11.master, ...), custom_call_target="tpu_custom_call" | custom-call | tf_op jit(solution)/shard_map/write_out/pallas_call | solution.py:417

commit v14 on v13

--- a/solution.py
+++ b/solution.py
@@ -37,7 +37,7 @@
     (0, N_TOP // 2, True), (N_TOP // 2, N_TOP - 2, True), (N_TOP - 2, N_TOP - 1, True), (N_TOP - 1, N_TOP, True),
 )
 STRIP = 1024
-UPDATE_STRIP = 3072
+UPDATE_STRIP = 2048
 
 TINY = 1.2e-38
 MIB = 1024 * 1024
@@ -62,14 +62,18 @@
     pltpu.make_async_copy(ref, ref, sem).wait()
 
 
-def row_views(array, shard, route, chunk, block, top):
+def slot(block, route, chunk, count=1):
+    return block.at[route, :, pl.ds(pl.multiple_of(chunk * COLS, COLS), count * COLS)]
+
+
+def row_views(array, shard, route, chunk, block, top, count=1):
     if top:
         start = shard * SHARD + route * TOP_ROUTE + chunk * COLS
-        return [(array.at[pl.ds(0, 8), pl.ds(pl.multiple_of(start, COLS), COLS)], block)]
+        return [(array.at[pl.ds(0, 8), pl.ds(pl.multiple_of(start, COLS), count * COLS)], block)]
     views = []
     for half in range(2):
         start = shard * SHARD + half * TOP_ROUTE + route * BOT_ROUTE + (chunk - N_TOP) * COLS
-        views.append((array.at[pl.ds(8, 4), pl.ds(pl.multiple_of(start, COLS), COLS)], block.at[pl.ds(4 * half, 4)]))
+        views.append((array.at[pl.ds(8, 4), pl.ds(pl.multiple_of(start, COLS), count * COLS)], block.at[pl.ds(4 * half, 4)]))
     return views
 
 
@@ -79,11 +83,11 @@
     return carry
 
 
-def strips(body, carry=0, width=STRIP):
+def strips(body, low, high, carry=0, width=STRIP):
     def step(strip, carry):
-        return body(pl.ds(pl.multiple_of(strip * width, width), width), carry)
-
-    return lax.fori_loop(0, COLS // width, step, carry)
+        return body(pl.ds(pl.multiple_of(low + strip * width, width), width), carry)
+
+    return lax.fori_loop(0, (high - low) // width, step, carry)
 
 
 def fold(total, values):
@@ -144,8 +148,8 @@
                     copy_to(src, dst, partner, first_send.at[int(top)], first_recv.at[route, index])
         return carry
 
-    def load(array, block, sem, route, chunk, top):
-        for src, dst in row_views(array, 0, route, chunk, block.at[route, chunk], top):
+    def load(array, block, sem, route, chunk, top, count=1):
+        for src, dst in row_views(array, 0, route, chunk, slot(block, route, chunk, count), top, count):
             pltpu.make_async_copy(src, dst, sem).start()
 
     next_to = [(model_pos, place) for chip in (1, 2) for place in (places[chip], data_index(*chips[chip], flip(core)))] + [(model_pos, partner), (flip(model_pos), places[0])]
@@ -161,29 +165,29 @@
     sweep(remote)
     tell(seen, next_to)
 
-    def load_state(chunk, carry, index, top):
-        for route in range(2):
-            load(master_in, master, load_sem.at[0], route, chunk, top)
-            load(one_in, one, load_sem.at[1], route, chunk, top)
-        return carry
-
-    sweep(load_state)
+    for index, (low, high, top) in enumerate(REDUCE_GROUPS):
+        for route in range(2):
+            load(master_in, master, load_sem.at[0], route, low, top, high - low)
+            load(one_in, one, load_sem.at[1], route, low, top, high - low)
     pl.semaphore_wait(seen, len(next_to))
     tell(known, next_to[-1:])
 
     def second(route, chunk, index):
-        copy_to(sent.at[route, chunk], got.at[route, chunk], places[2 - route], second_send, second_recv.at[route, index])
+        copy_to(slot(sent, route, chunk), slot(got, route, chunk), places[2 - route], second_send, second_recv.at[route, index])
 
     def add_four(chunk, squares, top):
         for route in range(2):
+            targets = [slot(block, route, chunk) for block in (mean, sent)]
+            weights_view = slot(master, route, chunk)
+
             def body(cols, total):
-                for far, target in ((0, mean), (1, sent)):
+                for far, target in enumerate(targets):
                     parts = [landing(route, chunk, 2 * source + far, 1, top)[:, cols].astype(F32) for source in range(4)]
-                    target[route, chunk, :, cols] = (parts[0] + parts[1]) + (parts[2] + parts[3])
-                weight = master[route, chunk, :, cols]
+                    target[:, cols] = (parts[0] + parts[1]) + (parts[2] + parts[3])
+                weight = weights_view[:, cols]
                 return fold(total, weight * weight)
 
-            squares = strips(body, squares)
+            squares = strips(body, 0, COLS, squares)
         return squares
 
     drain(master, load_sem.at[0])
@@ -200,23 +204,19 @@
             second(0, chunk, index)
             second(1, chunk, index)
 
-    def finish(chunk, squares, top):
-        for route in range(2):
-            def body(cols, total):
-                value = (mean[route, chunk, :, cols] + got[route, chunk, :, cols]) * 0.125
-                mean[route, chunk, :, cols] = value
-                return fold(total, value * value)
-
-            squares = strips(body, squares)
-            load(two_in, two, load_sem.at[2 + int(top)], route, chunk, top)
-        return squares
-
-    def finish_all():
+    def finish():
         squares = zero
         for index, (low, high, top) in enumerate(REDUCE_GROUPS):
             for route in range(2):
-                drain(got.at[route, pl.ds(low, high - low)], second_recv.at[route, index])
-            squares = lax.fori_loop(low, high, functools.partial(finish, top=top), squares)
+                drain(slot(got, route, low, high - low), second_recv.at[route, index])
+
+                def body(cols, total):
+                    value = (mean[route, :, cols] + got[route, :, cols]) * 0.125
+                    mean[route, :, cols] = value
+                    return fold(total, value * value)
+
+                squares = strips(body, low * COLS, high * COLS, squares)
+                load(two_in, two, load_sem.at[2 + int(top)], route, low, top, high - low)
         return squares
 
     everyone = [(row, data_index(*chip, side)) for row, chip in (
@@ -228,7 +228,7 @@
         for device in everyone:
             pltpu.make_async_remote_copy(src_ref=box.at[mine], dst_ref=box.at[mine], send_sem=send_sem, recv_sem=recv_sem, device_id=device, device_id_type=MESH).start()
 
-    total_box[mine] = jnp.sum(finish_all(), axis=0, keepdims=True)
+    total_box[mine] = jnp.sum(finish(), axis=0, keepdims=True)
     pl.semaphore_wait(known, 1)
     share_all(total_box, box_sem.at[0], box_sem.at[1])
     drain(total_box.at[pl.ds(0, 15)], box_sem.at[1])
@@ -236,9 +236,9 @@
     clip = jnp.minimum(1.0, MAX_NORM / jnp.sqrt(total))
     one_scale, two_scale = clip * (1.0 - BETA_ONE), clip * (1.0 - BETA_TWO) ** 0.5
 
-    def update(route, chunk, carry):
+    def update(route, low, high, carry):
         def body(cols, total):
-            place = (route, chunk, slice(None), cols)
+            place = (route, slice(None), cols)
             weight = master[place]
             value = mean[place]
             new_one = BETA_ONE * one[place] + one_scale * value
@@ -252,11 +252,11 @@
             mean[place] = direction
             return fold(total, direction * direction)
 
-        return strips(body, carry, UPDATE_STRIP)
+        return strips(body, low * COLS, high * COLS, carry, UPDATE_STRIP)
 
     def update_rows(index, low, high):
-        drain(two.at[:, pl.ds(low, high - low)], load_sem.at[2 + index])
-        return lax.fori_loop(low, high, lambda chunk, total: update(1, chunk, update(0, chunk, total)), zero)
+        drain(two.at[:, :, pl.ds(low * COLS, (high - low) * COLS)], load_sem.at[2 + index])
+        return update(1, low, high, update(0, low, high, zero))
 
     def share_norms(index, box, rows):
         for position, value in enumerate(rows):
@@ -298,15 +298,15 @@
 
     def weights(route, chunk, rate, top):
         view = piece(places[0], route, chunk, top)
+        masters, directions = slot(master, route, chunk), slot(mean, route, chunk)
 
         def body(cols, carry):
-            place = (route, chunk, slice(None), cols)
-            value = master[place] - rate * mean[place]
-            master[place] = value
+            value = masters[:, cols] - rate * directions[:, cols]
+            masters[:, cols] = value
             view[:, cols] = value.astype(BF16)
             return carry
 
-        strips(body)
+        strips(body, 0, COLS)
 
     def send(route, chunk, index, top):
         view = piece(places[0], route, chunk, top)
@@ -377,7 +377,7 @@
 
 def run_step(local_grads, master, moment_one, moment_two):
     dma = pltpu.SemaphoreType.DMA
-    block = pltpu.VMEM((2, N_CHUNK, 8, COLS), F32)
+    block = pltpu.VMEM((2, 8, N_CHUNK * COLS), F32)
     return pl.pallas_call(
         step_kernel,
         out_shape=(pltpu.VMEM((8, 8 * SHARD), BF16), pltpu.VMEM((8, 4 * SHARD), BF16), block, block, block),
@@ -404,8 +404,8 @@
             copies.append((bot.at[pl.ds(4 * half, 4), pl.ds(place * TOP_ROUTE, TOP_ROUTE)], params_out.at[pl.ds(8, 4), pl.ds(place * SHARD + half * TOP_ROUTE, TOP_ROUTE)]))
     for block, array in ((master, master_out), (one, one_out), (two, two_out)):
         for route in range(2):
-            for chunk in range(N_CHUNK):
-                copies += [(src, dst) for dst, src in row_views(array, 0, route, chunk, block.at[route, chunk], chunk < N_TOP)]
+            for first, count, top in ((0, N_TOP, True), (N_TOP, N_BOT, False)):
+                copies += [(src, dst) for dst, src in row_views(array, 0, route, first, slot(block, route, first, count), top, count)]
     for src, dst in copies:
         pltpu.make_async_copy(src, dst, sem).start()
     for src, dst in copies:

time: 377 us -> 377 us (level)
  no operation moved by 1% of the time
where the time goes in v14:
time: 377 us
  Pallas kernels  376 us (100%)
    pallas_call x1, Pallas kernels, run_step(): pl.pallas_call(step_kernel, out_shape=(pltpu.VMEM((8, 8 * SHARD), BF16),...  361 us
    pallas_call x1, Pallas kernels, write_out(): pl.pallas_call(write_kernel, out_shape=(jax.ShapeDtypeStruct((12, 8 * SHA...  15.7 us

profile of v14, /device:TPU:0, one launch (start us, length us, event | category | flops | bytes accessed | tf_op | source)
XLA Modules:
  0.0 377.1 jit_solution(3184081303724662817)
XLA Ops:
  0.6 360.7 %lamb_step.1 = (bf16[8,1179648]{1,0:T(8,128)(2,1)S(1)}, bf16[8,589824]{1,0:T(8,128)(2,1)S(1)}, f32[2,8,110592]{2,1,0:T(8,128)S(1)}, f32[2,8,110592]{2,1,0:T(8,128)S(1)}, f32[2,8,110592]{2,1,0:T(8,128)S(1)}) custom-call(bf16[1,12,1179648]{2,1,0:T(8,128)(2,1)} %grads.1, f32[12,147456]{1,0:T(8,128)} %master_in.1, f32[12,147456]{1,0:T(8,128)} %one_in.1, ...), custom_call_target="tpu_custom_call" | custom-call | tf_op jit(solution)/shard_map/lamb_step/pallas_call | solution.py:381
  361.3 15.7 %write_out.1 = (bf16[12,1179648]{1,0:T(8,128)(2,1)}, f32[12,147456]{1,0:T(8,128)}, f32[12,147456]{1,0:T(8,128)}, f32[12,147456]{1,0:T(8,128)}) custom-call(bf16[8,1179648]{1,0:T(8,128)(2,1)S(1)} %get-tuple-element.9.top, bf16[8,589824]{1,0:T(8,128)(2,1)S(1)} %get-tuple-element.10.bot, f32[2,8,110592]{2,1,0:T(8,128)S(1)} %get-tuple-element.11.master, ...), custom_call_target="tpu_custom_call" | custom-call | tf_op jit(solution)/shard_map/write_out/pallas_call | solution.py:417

commit v15 on v13

--- a/solution.py
+++ b/solution.py
@@ -231,19 +231,30 @@
     total_box[mine] = jnp.sum(finish_all(), axis=0, keepdims=True)
     pl.semaphore_wait(known, 1)
     share_all(total_box, box_sem.at[0], box_sem.at[1])
+
+    drain(one, load_sem.at[1])
+    drain(two.at[:, pl.ds(N_TOP, N_BOT)], load_sem.at[2])
+
+    @pl.loop(N_TOP, N_CHUNK)
+    def _(chunk):
+        for route in range(2):
+            for block, rate in ((one, BETA_ONE), (two, BETA_TWO)):
+                block[route, chunk] = rate * block[route, chunk]
+
     drain(total_box.at[pl.ds(0, 15)], box_sem.at[1])
     total = jnp.sum(jnp.sum(total_box[...], axis=0), keepdims=True)
     clip = jnp.minimum(1.0, MAX_NORM / jnp.sqrt(total))
     one_scale, two_scale = clip * (1.0 - BETA_ONE), clip * (1.0 - BETA_TWO) ** 0.5
 
-    def update(route, chunk, carry):
+    def update(route, chunk, carry, decayed):
         def body(cols, total):
             place = (route, chunk, slice(None), cols)
             weight = master[place]
             value = mean[place]
-            new_one = BETA_ONE * one[place] + one_scale * value
+            old_one, old_two = (one[place], two[place]) if decayed else (BETA_ONE * one[place], BETA_TWO * two[place])
+            new_one = old_one + one_scale * value
             change = two_scale * value
-            new_two = BETA_TWO * two[place] + change * change
+            new_two = old_two + change * change
             one[place] = new_one
             two[place] = new_two
             floor = jnp.maximum(new_two, TINY)
@@ -255,8 +266,7 @@
         return strips(body, carry, UPDATE_STRIP)
 
     def update_rows(index, low, high):
-        drain(two.at[:, pl.ds(low, high - low)], load_sem.at[2 + index])
-        return lax.fori_loop(low, high, lambda chunk, total: update(1, chunk, update(0, chunk, total)), zero)
+        return lax.fori_loop(low, high, lambda chunk, total: update(1, chunk, update(0, chunk, total, index == 0), index == 0), zero)
 
     def share_norms(index, box, rows):
         for position, value in enumerate(rows):
@@ -281,8 +291,8 @@
         row = lax.broadcasted_iota(jnp.int32, (8, 128), 0)
         return [jnp.sum(jnp.where(mask, squares, 0.0), axis=0, keepdims=True) for mask in (row < 3, row == 3, row > 3)]
 
-    drain(one, load_sem.at[1])
     share_norms(0, bot_box, [jnp.sum(squares, axis=0, keepdims=True) for squares in (bot_squares, update_rows(0, N_TOP, N_CHUNK))])
+    drain(two.at[:, pl.ds(0, N_TOP)], load_sem.at[3])
     share_norms(1, top_box, tensor_rows(top_squares) + tensor_rows(update_rows(1, 0, N_TOP)))
 
     def piece(place, route, chunk, top, count=1):

time: 377 us -> 377 us (level)
  no operation moved by 1% of the time
where the time goes in v15:
time: 377 us; the launch traced here: 376 us
  Pallas kernels  376 us (100%)
    pallas_call x1, Pallas kernels, run_step(): pl.pallas_call(step_kernel, out_shape=(pltpu.VMEM((8, 8 * SHARD), BF16),...  360 us
    pallas_call x1, Pallas kernels, write_out(): pl.pallas_call(write_kernel, out_shape=(jax.ShapeDtypeStruct((12, 8 * SHA...  15.7 us

profile of v15, /device:TPU:0, one launch (start us, length us, event | category | flops | bytes accessed | tf_op | source)
XLA Modules:
  0.0 376.4 jit_solution(7568288271083471358)
XLA Ops:
  0.6 360.1 %lamb_step.1 = (bf16[8,1179648]{1,0:T(8,128)(2,1)S(1)}, bf16[8,589824]{1,0:T(8,128)(2,1)S(1)}, f32[2,36,8,3072]{3,2,1,0:T(8,128)S(1)}, f32[2,36,8,3072]{3,2,1,0:T(8,128)S(1)}, f32[2,36,8,3072]{3,2,1,0:T(8,128)S(1)}) custom-call(bf16[1,12,1179648]{2,1,0:T(8,128)(2,1)} %grads.1, f32[12,147456]{1,0:T(8,128)} %master_in.1, f32[12,147456]{1,0:T(8,128)} %one_in.1, ...), custom_call_target="tpu_custom_call" | custom-call | tf_op jit(solution)/shard_map/lamb_step/pallas_call | solution.py:391
  360.8 15.7 %write_out.1 = (bf16[12,1179648]{1,0:T(8,128)(2,1)}, f32[12,147456]{1,0:T(8,128)}, f32[12,147456]{1,0:T(8,128)}, f32[12,147456]{1,0:T(8,128)}) custom-call(bf16[8,1179648]{1,0:T(8,128)(2,1)S(1)} %get-tuple-element.9.top, bf16[8,589824]{1,0:T(8,128)(2,1)S(1)} %get-tuple-element.10.bot, f32[2,36,8,3072]{3,2,1,0:T(8,128)S(1)} %get-tuple-element.11.master, ...), custom_call_target="tpu_custom_call" | custom-call | tf_op jit(solution)/shard_map/write_out/pallas_call | solution.py:427
